TPU v7x, 32 devices: a whole 2x2x4 slice. The times are simulated.
32 devices in a mesh: grp: 2 (over y), ctx: 8 (over z, x), head: 2 (over core).
Axes of the slice: x: 2, y: 2, z: 4, core: 2. Of those that a mesh axis runs over, the one named last changes fastest.
Arguments:
- block_owner: int32 [32, 1], P('grp'), parts along dimension 0, may hold values from 0 to 7; in each aligned block of 16 rows (0 to 15, 16 to 31, ...) at most 6 rows name the same one
- block_slot: int32 [32], P('grp'), parts along dimension 0, may hold values from 0 to 1
- recv_keys: bfloat16 [4096, 1024], P(('grp', 'ctx'), 'head'), parts along dimension 0, may hold values from -4.5 to 4.5
- recv_values: bfloat16 [4096, 1024], P(('grp', 'ctx'), 'head'), parts along dimension 0, may hold values from -6 to 6
- sharer_values: bfloat16 [4096, 1024], P(('grp', 'ctx'), 'head'), parts along dimension 0, may hold values from -6 to 6
- queries: bfloat16 [16, 8192], P(('grp', 'ctx'), 'head'), parts along dimension 0, may hold values from -170 to 170
- new_keys: bfloat16 [16, 1024], P(('grp', 'ctx'), 'head'), parts along dimension 0, may hold values from -7 to 7
- new_values: bfloat16 [16, 1024], P(('grp', 'ctx'), 'head'), parts along dimension 0, may hold values from -6 to 6
- mixer_gate: bfloat16 [256, 2048], replicated, may hold values from -0.375 to 0.375
- mixer_up: bfloat16 [256, 2048], replicated, may hold values from -0.375 to 0.375
- mixer_down: bfloat16 [2048, 128], replicated, may hold values from -0.125 to 0.125
- gate_logit: float32 [8], P('head'), may hold values from -2 to 2
Outputs:
- merged_values: bfloat16 [4096, 1024], P(('grp', 'ctx'), 'head'), parts along dimension 0
- attended: bfloat16 [16, 8192], P(('grp', 'ctx'), 'head'), parts along dimension 0
There are 2 independent parts, one for each index of `grp`. A program takes and returns all parts, laid end to end along the dimension named above; an argument that names none is the same for every part. Nothing has to cross between parts.
Inputs may be any that keep to these rules, and one draw needn't show every extreme that they name: `block_owner`: every owner is named by at least one sharer block and by at most 6; some owner by exactly 6.
All inputs are finite; a program needn't handle non-finite values.
Results may differ from a plain program's by a relative error of at most 0.0053.
Values may be sent and summed in bfloat16 or wider, within the bound.
No kernel may reach another device: no remote copies, remote signals or barrier semaphores. Data moves between devices by JAX's collectives and lax.ppermute only.
A program may use at most 64 MiB of HBM per device.

v0:
```python
import math

import jax
import jax.numpy as jnp
from jax import lax
from jax.sharding import PartitionSpec as P

DH = 128
BLK = 128


def mixer_block(value_block, aligned_block, mixer_gate, mixer_up, mixer_down, head_gates):
    row_count = value_block.shape[0] * value_block.shape[1]
    joined = jnp.concatenate([value_block, aligned_block], axis=2).reshape(
        row_count, 2 * value_block.shape[2]
    )
    gate_pre = jnp.dot(joined, mixer_gate, preferred_element_type=jnp.float32)
    up_pre = jnp.dot(joined, mixer_up, preferred_element_type=jnp.float32)
    hidden = (jax.nn.silu(gate_pre) * up_pre).astype(jnp.bfloat16)
    update = jnp.dot(hidden, mixer_down, preferred_element_type=jnp.float32).reshape(
        value_block.shape
    )
    merged = value_block.astype(jnp.float32) + head_gates[None, :, None] * update
    return merged.astype(jnp.bfloat16)


def body(
    block_owner,
    block_slot,
    recv_keys,
    recv_values,
    sharer_values,
    queries,
    new_keys,
    new_values,
    mixer_gate,
    mixer_up,
    mixer_down,
    gate_logit,
):
    ctx_count = lax.axis_size("ctx")
    ctx_place = lax.axis_index("ctx")
    col_width = recv_values.shape[1]
    heads_here = col_width // DH
    tokens = recv_values.shape[0]
    blocks_here = tokens // BLK
    blocks_all = blocks_here * ctx_count
    slice_len = BLK // ctx_count
    cap_slots = min(3 * blocks_here, ctx_count * blocks_here // 2)
    owner_list = block_owner[:, 0]
    block_ids = jnp.arange(blocks_all, dtype=jnp.int32)
    pieces = sharer_values.reshape(blocks_here, ctx_count, slice_len, col_width)
    relayed = lax.all_to_all(pieces, "ctx", split_axis=1, concat_axis=0, tiled=True)
    relayed = relayed.reshape(blocks_all, slice_len * col_width)
    same_owner = owner_list[None, :] == owner_list[:, None]
    earlier = block_ids[None, :] < block_ids[:, None]
    block_rank = jnp.sum((same_owner & earlier).astype(jnp.int32), axis=1)
    slot_index = owner_list * cap_slots + block_rank
    padded = (
        jnp.zeros((ctx_count * cap_slots, slice_len * col_width), jnp.bfloat16)
        .at[slot_index]
        .set(relayed)
    )
    padded = padded.reshape(ctx_count, cap_slots, 1, slice_len, col_width)
    arrived = lax.all_to_all(padded, "ctx", split_axis=0, concat_axis=2, tiled=True)
    incoming = arrived.reshape(cap_slots, BLK * col_width)
    own_blocks = owner_list == ctx_place
    rank_hot = (
        (block_rank[:, None] == jnp.arange(cap_slots)[None, :]) & own_blocks[:, None]
    ).astype(jnp.float32)
    slot_hot = (block_slot[:, None] == jnp.arange(blocks_here)[None, :]).astype(jnp.float32)
    routing = jnp.dot(slot_hot.T, rank_hot, precision=lax.Precision.HIGHEST)
    counts = jnp.sum(routing, axis=1)
    block_sums = jnp.dot(routing.astype(jnp.bfloat16), incoming, preferred_element_type=jnp.float32)
    aligned = (
        (block_sums / jnp.maximum(counts, 1.0)[:, None])
        .astype(jnp.bfloat16)
        .reshape(tokens, col_width)
    )
    value_blocks = recv_values.reshape(blocks_here, BLK, heads_here, DH)
    aligned_blocks = aligned.reshape(blocks_here, BLK, heads_here, DH)
    head_gates = jax.nn.sigmoid(gate_logit)

    def blend_pair(block_pair):
        return mixer_block(
            block_pair[0], block_pair[1], mixer_gate, mixer_up, mixer_down, head_gates
        )

    merged = lax.map(blend_pair, (value_blocks, aligned_blocks)).reshape(tokens, col_width)
    all_queries, all_new_keys, all_new_values = (
        lax.all_gather(queries, "ctx", axis=0, tiled=True),
        lax.all_gather(new_keys, "ctx", axis=0, tiled=True),
        lax.all_gather(new_values, "ctx", axis=0, tiled=True),
    )
    rows_all = all_queries.shape[0]
    rows_mine = queries.shape[0]
    groups = queries.shape[1] // col_width
    score_scale = 1.0 / math.sqrt(DH)
    query_heads = all_queries.reshape(rows_all, heads_here, groups, DH)
    key_heads = recv_keys.reshape(tokens, heads_here, DH)
    scores = (
        jnp.einsum("qhgd,khd->qhgk", query_heads, key_heads, preferred_element_type=jnp.float32)
        * score_scale
    )
    fresh = (
        jnp.einsum(
            "qhgd,uhd->qhgu",
            query_heads,
            all_new_keys.reshape(rows_all, heads_here, DH),
            preferred_element_type=jnp.float32,
        )
        * score_scale
    )
    causal = jnp.arange(rows_all)[None, :] <= jnp.arange(rows_all)[:, None]
    fresh = jnp.where(causal[:, None, None, :], fresh, -jnp.inf)
    cache_top = lax.pmax(jnp.max(scores, axis=3), "ctx")
    row_top = jnp.maximum(cache_top, jnp.max(fresh, axis=3))
    weights = jnp.exp(scores - row_top[..., None])
    denom_part = jnp.sum(weights, axis=3)
    numer_part = jnp.einsum(
        "qhgk,khd->qhgd",
        weights.astype(jnp.bfloat16),
        merged.reshape(tokens, heads_here, DH),
        preferred_element_type=jnp.float32,
    )
    row_start = ctx_place * rows_mine
    fresh_mine = jnp.exp(
        lax.dynamic_slice_in_dim(fresh, row_start, rows_mine, 0)
        - lax.dynamic_slice_in_dim(row_top, row_start, rows_mine, 0)[..., None]
    )
    fresh_den = jnp.sum(fresh_mine, axis=3)
    fresh_num = jnp.einsum(
        "qhgu,uhd->qhgd",
        fresh_mine.astype(jnp.bfloat16),
        all_new_values.reshape(rows_all, heads_here, DH),
        preferred_element_type=jnp.float32,
    )
    numer_all, denom_all = lax.psum((numer_part, denom_part), "ctx")
    numer_rows = lax.dynamic_slice_in_dim(numer_all, row_start, rows_mine, 0)
    denom_rows = lax.dynamic_slice_in_dim(denom_all, row_start, rows_mine, 0)
    attended = ((numer_rows + fresh_num) / (denom_rows + fresh_den)[..., None]).astype(jnp.bfloat16)
    return (merged, attended.reshape(rows_mine, heads_here * groups * DH))


def solution(mesh):
    return jax.shard_map(
        body,
        mesh=mesh,
        in_specs=(
            P("grp", None),
            P("grp"),
            P(("grp", "ctx"), "head"),
            P(("grp", "ctx"), "head"),
            P(("grp", "ctx"), "head"),
            P(("grp", "ctx"), "head"),
            P(("grp", "ctx"), "head"),
            P(("grp", "ctx"), "head"),
            P(),
            P(),
            P(),
            P("head"),
        ),
        out_specs=(P(("grp", "ctx"), "head"), P(("grp", "ctx"), "head")),
        check_vma=False,
    )
```

profile of v0, /device:TPU:0, one launch (start us, length us, event | category | flops | bytes accessed | tf_op | source)
XLA Modules:
  0.0 279.4 jit_solution(1551210746189556537)
XLA Ops:
  7.2 0.0 copy-start.3
  7.2 1.7 copy.44
  8.9 7.3 %all-to-all-start = ((bf16[2,8,16,512]{3,2,0,1:T(8,128)(2,1)}), bf16[2,8,16,512]{3,2,0,1:T(8,128)(2,1)S(1)}, u32[]{:S(2)}, u32[]{:S(2)}) async-start(bf16[2,8,16,512]{3,2,0,1:T(8,128)(2,1)} %copy.44), calls=%async_computation | async-start | bytes 524288 | tf_op jit(solution)/shard_map/all_to_all | solution.py:53
  16.2 1.0 reshape.94
  17.2 32.0 %all-gather = bf16[8,1,4096]{2,1,0:T(2,128)(2,1)S(1)} all-gather(bf16[1,1,4096]{2,1,0:T(2,128)(2,1)} %bitcast.130), channel_id=1, replica_groups=mesh['grp'=2,'ctx'=8,'head'=2] {'ctx'}, dimensions={0}, use_global_device_ids=true | all-gather | bytes 73728 | tf_op jit(solution)/shard_map/all_gather | solution.py:91
  49.2 0.4 reduce.1
  49.5 0.3 fusion.44
  49.8 1.0 reshape.88
  50.9 36.4 %pmax.7 = f32[8,4,8]{2,0,1:T(8,128)S(1)} all-reduce(f32[8,4,8]{2,0,1:T(8,128)S(1)} %get-tuple-element.65), channel_id=1, replica_groups=mesh['grp'=2,'ctx'=8,'head'=2] {'ctx'}, use_global_device_ids=true, to_apply=%region_6.7 | all-reduce | flops 256 | bytes 2048 | tf_op jit(solution)/shard_map/pmax | solution.py:116
  87.3 26.5 %all-gather.1 = bf16[8,1,512]{2,1,0:T(2,128)(2,1)S(1)} all-gather(bf16[1,1,512]{2,1,0:T(2,128)(2,1)} %bitcast.134), channel_id=1, replica_groups=mesh['grp'=2,'ctx'=8,'head'=2] {'ctx'}, dimensions={0}, use_global_device_ids=true | all-gather | bytes 9216 | tf_op jit(solution)/shard_map/all_gather | solution.py:92
  113.8 0.9 convert_reduce_fusion
  114.7 0.7 fusion.41
  115.4 0.0 all-to-all-done
  115.4 0.1 copy.63
  115.5 1.2 scatter_custom_fusion
  116.8 1.1 copy.64
  117.9 3.5 %all-to-all-start.1 = ((bf16[8,6,1,16,512]{4,3,1,2,0:T(8,128)(2,1)}), bf16[8,6,1,16,512]{4,3,1,2,0:T(8,128)(2,1)S(1)}, u32[]{:S(2)}, u32[]{:S(2)}) async-start(bf16[8,6,1,16,512]{4,3,1,2,0:T(8,128)(2,1)} %bitcast.10), calls=%async_computation.1 | async-start | bytes 1572864 | tf_op jit(solution)/shard_map/all_to_all | solution.py:65
  121.5 0.0 all-reduce.2.cloned.1.call-start
  121.5 0.4 fusion.45
  121.9 0.2 fusion.18
  122.2 37.6 %psum.15 = f32[8,4,8]{2,0,1:T(8,128)S(1)} all-reduce(f32[8,4,8]{2,0,1:T(8,128)S(1)} %fusion.18), channel_id=1, replica_groups=mesh['grp'=2,'ctx'=8,'head'=2] {'ctx'}, use_global_device_ids=true, to_apply=%region_10.11 | all-reduce | flops 256 | bytes 2048 | tf_op jit(solution)/shard_map/psum | solution.py:138
  159.7 26.1 %all-gather.2 = bf16[8,1,512]{2,1,0:T(2,128)(2,1)S(1)} all-gather(bf16[1,1,512]{2,1,0:T(2,128)(2,1)S(1)} %bitcast.135), channel_id=1, replica_groups=mesh['grp'=2,'ctx'=8,'head'=2] {'ctx'}, dimensions={0}, use_global_device_ids=true | all-gather | bytes 9216 | tf_op jit(solution)/shard_map/all_gather | solution.py:93
  185.9 0.0 copy-done.5
  185.9 0.4 fusion.43
  186.3 0.0 all-to-all-done.1
  186.3 0.1 copy.46
  186.4 0.9 reshape.92
  187.3 0.0 copy-start
  187.3 0.4 fusion.7
  187.7 0.2 reshape_reshape.6
  188.0 0.6 copy-done
  188.5 13.6 %while.10 = (s32[]{:T(128)}, bf16[2,128,4,128]{3,2,1,0:T(4,128)(2,1)S(1)}, bf16[2,128,4,128]{3,2,1,0:T(4,128)(2,1)S(1)}, f32[4]{0:T(128)S(1)}, bf16[2,128,4,128]...) while((s32[]{:T(128)}, ...), condition=%wide.region_4.5_spmd, body=%wide.region_3.4_spmd.sunk | while | flops 1349779456 | bytes 14942857 | solution.py:89
  188.5 0.1 constant_dynamic-slice_fusion.4
  188.6 2.6 fusion.60
  191.3 3.9 %fusion.61 = f32[512,128]{1,0:T(8,128)S(1)} fusion(bf16[2048,128]{1,0:T(8,128)(2,1)S(1)} %copy-done.2, f32[512,2048]{1,0:T(8,128)} %fusion.60, bf16[256,2048]{1,0:T(8,128)(2,1)} %get-tuple-element.148, bf16[512,128]{1,0:T(8,128)(2,1)S(1)} %bitcast.115, bf16[512,128]{1,0:T(8,128)(2,1)S(1)} %bitcast.117), kind=kOutput, calls=%fused_computation.2.clone.1 | convolution fusion | flops 812122112 | bytes 6291456 | tf_op jit(solution)/shard_map/while/body/eval_jaxpr/dot_general | solution.py:20
  195.2 0.2 fusion.62
  195.3 0.0 copy-start.2
  195.3 0.1 constant_dynamic-slice_fusion.4
  195.5 2.6 fusion.60
  198.1 0.0 copy-done.2
  198.1 3.9 %fusion.61 = f32[512,128]{1,0:T(8,128)S(1)} fusion(bf16[2048,128]{1,0:T(8,128)(2,1)S(1)} %copy-done.2, f32[512,2048]{1,0:T(8,128)} %fusion.60, bf16[256,2048]{1,0:T(8,128)(2,1)} %get-tuple-element.148, bf16[512,128]{1,0:T(8,128)(2,1)S(1)} %bitcast.115, bf16[512,128]{1,0:T(8,128)(2,1)S(1)} %bitcast.117), kind=kOutput, calls=%fused_computation.2.clone.1 | convolution fusion | flops 812122112 | bytes 6291456 | tf_op jit(solution)/shard_map/while/body/eval_jaxpr/dot_general | solution.py:20
  202.0 0.2 fusion.62
  202.1 0.9 convolution_bitcast_fusion
  203.0 0.0 all-reduce.2.cloned.1.call-update
  203.1 0.7 copy.97
  203.8 67.2 %all-reduce.2.cloned.1.call-done = f32[8,4,8,128]{3,2,0,1:T(8,128)} async-done(((f32[8,4,8,128]{3,2,0,1:T(8,128)}), f32[8,4,8,128]{3,2,0,1:T(8,128)}) %all-reduce.2.cloned.1.call-update) | async-done | bytes 131088 | tf_op jit(solution)/shard_map/psum | solution.py:138
  271.0 0.9 fusion.13
  271.9 0.7 reshape.99
  (17 shorter events, 0.1 us)
Async XLA Ops:
  7.2 178.7 %copy-start.3 = (s32[16,1]{0,1:T(1,128)S(1)}, s32[16,1]{0,1:T(1,128)}, u32[]{:S(2)}) copy-start(s32[16,1]{0,1:T(1,128)} %param.14) | copy-start | bytes 196
  7.2 152.6 %copy-start.1 = (bf16[1,512]{1,0:T(2,128)(2,1)S(1)}, bf16[1,512]{1,0:T(2,128)(2,1)}, u32[]{:S(2)}) copy-start(bf16[1,512]{1,0:T(2,128)(2,1)} %param.21) | copy-start | bytes 3076
  7.2 178.7 %copy-start.4 = (f32[4]{0:T(128)S(1)}, f32[4]{0:T(128)}, u32[]{:S(2)}) copy-start(f32[4]{0:T(128)} %param.25) | copy-start | bytes 52
  7.2 178.7 %copy-start.5 = (s32[16]{0:T(128)S(1)}, s32[16]{0:T(128)}, u32[]{:S(2)}) copy-start(s32[16]{0:T(128)} %param.15) | copy-start | bytes 196
  8.9 106.5 %all-to-all-start = ((bf16[2,8,16,512]{3,2,0,1:T(8,128)(2,1)}), bf16[2,8,16,512]{3,2,0,1:T(8,128)(2,1)S(1)}, u32[]{:S(2)}, u32[]{:S(2)}) async-start(bf16[2,8,16,512]{3,2,0,1:T(8,128)(2,1)} %copy.44), calls=%async_computation | async-start | bytes 524288 | tf_op jit(solution)/shard_map/all_to_all | solution.py:53
  117.9 68.4 %all-to-all-start.1 = ((bf16[8,6,1,16,512]{4,3,1,2,0:T(8,128)(2,1)}), bf16[8,6,1,16,512]{4,3,1,2,0:T(8,128)(2,1)S(1)}, u32[]{:S(2)}, u32[]{:S(2)}) async-start(bf16[8,6,1,16,512]{4,3,1,2,0:T(8,128)(2,1)} %bitcast.10), calls=%async_computation.1 | async-start | bytes 1572864 | tf_op jit(solution)/shard_map/all_to_all | solution.py:65
  121.5 149.5 %all-reduce.2.cloned.1.call-start = ((), (), s32[]{:S(2)}) async-start(), calls=%async_computation.2 | async-start | bytes 262144 | tf_op jit(solution)/shard_map/psum | solution.py:138
  187.3 1.2 copy-start
  188.5 2.7 copy-start.2
  195.3 2.8 copy-start.2
Sparse Core Ops, SparseCore 0:
  203.2 67.7 all-reduce.1
where the time goes:
time: 280 us; the launch traced here: 279 us
  blocking collectives  159 us (57%)
  waiting for transfers between devices  67.2 us (24%)
  matrix products  16.2 us (6%)
  between operations  14.2 us (5%)
  starting transfers between devices  10.9 us (4%)
  local copies, waits for them, and re-layouts  9.63 us (3%)
    psum x1, waiting for transfers between devices, body(): numer_all, denom_all = lax.psum((numer_part, denom_part), 'ctx')  67.2 us
    psum x1, blocking collectives, body(): numer_all, denom_all = lax.psum((numer_part, denom_part), 'ctx')  37.6 us
    pmax x1, blocking collectives, body(): cache_top = lax.pmax(jnp.max(scores, axis=3), 'ctx')  36.4 us
    all_gather x1, blocking collectives, body(): lax.all_gather(queries, 'ctx', axis=0, tiled=True)  32 us
    all_gather x1, blocking collectives, body(): lax.all_gather(new_keys, 'ctx', axis=0, tiled=True)  26.5 us
    all_gather x1, blocking collectives, body(): lax.all_gather(new_values, 'ctx', axis=0, tiled=True)  26.1 us
    dot_general x2, matrix products, mixer_block(): jnp.dot(hidden, mixer_down, preferred_element_type=jnp.float32)  7.73 us
    all_to_all x1, starting transfers between devices, body(): lax.all_to_all(pieces, 'ctx', split_axis=1, concat_axis=0, tiled=True)  7.28 us
  transfers between devices with their start and end apart: 3, of which 1 were waited for; matrix products, arithmetic and copies ran while one was open for 2% of the time, Pallas kernels for 0%

commit v1 on v0

v1 whole, which is shorter than its diff:
```python
import functools
import math

import jax
import jax.numpy as jnp
from jax import lax
from jax.experimental import pallas as pl
from jax.experimental.pallas import tpu as pltpu
from jax.sharding import PartitionSpec as P

DH = 128
BLK = 128
G = 8
STAT = 8
NEG = -1e30
SMEM = pl.BlockSpec(memory_space=pltpu.SMEM)
VMEM = pl.BlockSpec(memory_space=pltpu.VMEM)


def exchange(x):
    return lax.all_to_all(x, "ctx", split_axis=0, concat_axis=0, tiled=True)


def query_tile(query_ref, scratch):
    for r in range(scratch.shape[0]):
        scratch[r : r + 1, :] = query_ref[0:1, r * DH : (r + 1) * DH].astype(jnp.float32)
    return scratch[...].astype(jnp.bfloat16)


def pack_kernel(sharer_ref, query_ref, out_ref, scratch, *, blocks, slice_len):
    devices = out_ref.shape[0]
    width = sharer_ref.shape[1]
    q = query_tile(query_ref, scratch)
    for d in range(devices):
        for k in range(blocks):
            start = k * BLK + d * slice_len
            out_ref[d, k * slice_len : (k + 1) * slice_len, :width] = sharer_ref[
                start : start + slice_len, :
            ]
        out_ref[d, :, width:] = q


def align_kernel(owner_ref, slot_ref, got_ref, out_ref, sums, counts, *, blocks, slice_len):
    devices = out_ref.shape[0]
    width = out_ref.shape[2]
    total = devices * blocks
    sums[...] = jnp.zeros(sums.shape, jnp.float32)
    for r in range(total):
        counts[r] = 0
    for b in range(total):
        dest = owner_ref[b] * blocks + slot_ref[b]
        s, k = divmod(b, blocks)
        sums[dest] += got_ref[s, k * slice_len : (k + 1) * slice_len, :width].astype(jnp.float32)
        counts[dest] = counts[dest] + 1
    for r in range(total):
        d, k = divmod(r, blocks)
        many = jnp.full((1, width), jnp.maximum(counts[r], 1), jnp.int32).astype(jnp.float32)
        out_ref[d, k * slice_len : (k + 1) * slice_len, :] = (sums[r] / many).astype(jnp.bfloat16)


def score_kernel(place_ref, got_ref, key_ref, new_key_ref, new_value_ref, weight_ref, part_ref, *, heads):
    rows = got_ref.shape[0]
    scale = 1.0 / math.sqrt(DH)
    q_all = got_ref[:, :, got_ref.shape[2] - DH :].astype(jnp.float32)
    row_of = lax.broadcasted_iota(jnp.int32, (rows * G, 1), 0) // G
    allowed = row_of >= place_ref[0]
    sub = lax.broadcasted_iota(jnp.int32, (1, G, DH), 1)
    lane = lax.broadcasted_iota(jnp.int32, (1, G, DH), 2)
    tops = jnp.zeros((rows, 1, DH), jnp.float32)
    dens = jnp.zeros((rows, 1, DH), jnp.float32)
    for j in range(heads):
        cols = slice(j * DH, (j + 1) * DH)
        q = q_all[:, j * G : (j + 1) * G, :].reshape(rows * G, DH)
        s = (
            lax.dot_general(
                q.astype(jnp.bfloat16),
                key_ref[:, cols],
                (((1,), (1,)), ((), ())),
                preferred_element_type=jnp.float32,
            )
            * scale
        )
        sf = jnp.sum(q * new_key_ref[0:1, cols].astype(jnp.float32), axis=1, keepdims=True) * scale
        top = jnp.maximum(
            jnp.max(s, axis=1, keepdims=True), jnp.where(allowed, sf, NEG)
        )
        w = jnp.exp(s - top)
        wf = jnp.where(allowed, jnp.exp(jnp.where(allowed, sf, top) - top), 0.0)
        den = jnp.sum(w, axis=1, keepdims=True) + wf
        weight_ref[j] = w.astype(jnp.bfloat16)
        fresh = wf.astype(jnp.bfloat16).astype(jnp.float32) * new_value_ref[0:1, cols].astype(
            jnp.float32
        )
        part_ref[:, j * G : (j + 1) * G, :] = fresh.reshape(rows, G, DH)
        here = lane == sub + j * G
        spread = lambda v: jnp.sum(
            jnp.where(here, jnp.broadcast_to(v, (rows * G, DH)).reshape(rows, G, DH), 0.0),
            axis=1,
            keepdims=True,
        )
        tops += spread(top)
        dens += spread(den)
    part_ref[:, heads * G :, :] = jnp.where(
        sub == 0, jnp.broadcast_to(tops, (rows, STAT, DH)), jnp.broadcast_to(dens, (rows, STAT, DH))
    )


def mixer_kernel(
    logit_ref, got_ref, value_ref, gate_ref, up_ref, down_ref, weight_ref, part_ref, merged_ref, out_ref,
    *, blocks, slice_len, chunk
):
    tokens, width = value_ref.shape
    heads = width // DH
    hidden = gate_ref.shape[1]
    rows = part_ref.shape[0]
    out_ref[:, heads * G :, :] = part_ref[:, heads * G :, :]
    for j in range(heads):
        cols = slice(j * DH, (j + 1) * DH)
        v = value_ref[:, cols]
        if slice_len:
            a = jnp.concatenate(
                [
                    got_ref[s, k * slice_len : (k + 1) * slice_len, cols]
                    for k in range(blocks)
                    for s in range(got_ref.shape[0])
                ],
                axis=0,
            )
        else:
            a = got_ref[:, cols]
        x = jnp.concatenate([v, a], axis=1)
        update = jnp.zeros((tokens, DH), jnp.float32)
        for c in range(0, hidden, chunk):
            g = jnp.dot(x, gate_ref[:, c : c + chunk], preferred_element_type=jnp.float32)
            u = jnp.dot(x, up_ref[:, c : c + chunk], preferred_element_type=jnp.float32)
            half = g * 0.5
            h = ((half + half * jnp.tanh(half)) * u).astype(jnp.bfloat16)
            update += jnp.dot(h, down_ref[c : c + chunk, :], preferred_element_type=jnp.float32)
        head_gate = jax.nn.sigmoid(jnp.full((1, DH), logit_ref[j], jnp.float32))
        merged = (v.astype(jnp.float32) + head_gate * update).astype(jnp.bfloat16)
        merged_ref[:, cols] = merged
        numer = jnp.dot(weight_ref[j], merged, preferred_element_type=jnp.float32)
        out_ref[:, j * G : (j + 1) * G, :] = part_ref[:, j * G : (j + 1) * G, :] + numer.reshape(
            rows, G, DH
        )


def combine_kernel(got_ref, out_ref, scratch, *, heads):
    n = heads * G
    tops = got_ref[:, n : n + 1, :]
    dens = got_ref[:, n + 1 : n + 2, :]
    factor = jnp.exp(tops - jnp.max(tops, axis=0, keepdims=True))
    factor = factor / jnp.sum(factor * dens, axis=0, keepdims=True)
    sub = lax.broadcasted_iota(jnp.int32, (1, n, DH), 1)
    lane = lax.broadcasted_iota(jnp.int32, (1, n, DH), 2)
    column = jnp.sum(jnp.where(lane == sub, factor, 0.0), axis=2, keepdims=True)
    scratch[...] = jnp.sum(column * got_ref[:, :n, :], axis=0)
    for r in range(n):
        out_ref[0:1, r * DH : (r + 1) * DH] = scratch[r : r + 1, :].astype(jnp.bfloat16)


def body(
    block_owner, block_slot, recv_keys, recv_values, sharer_values, queries, new_keys, new_values,
    mixer_gate, mixer_up, mixer_down, gate_logit,
):
    devices = lax.axis_size("ctx")
    place = lax.axis_index("ctx").astype(jnp.int32).reshape(1)
    tokens, width = recv_values.shape
    heads = width // DH
    blocks = tokens // BLK
    total = blocks * devices
    slice_len = BLK // devices
    owner = block_owner[:, 0]
    rows = devices
    tiled = slice_len % 16 == 0
    f32, bf16 = jnp.float32, jnp.bfloat16
    shape = jax.ShapeDtypeStruct

    if tiled:
        send = pl.pallas_call(
            functools.partial(pack_kernel, blocks=blocks, slice_len=slice_len),
            out_shape=shape((devices, blocks * slice_len, width + DH), bf16),
            scratch_shapes=[pltpu.VMEM((heads * G, DH), f32)],
            name="pack",
        )(sharer_values, queries)
        got = exchange(send)
        mean = pl.pallas_call(
            functools.partial(align_kernel, blocks=blocks, slice_len=slice_len),
            out_shape=shape((devices, blocks * slice_len, width), bf16),
            in_specs=[SMEM, SMEM, VMEM],
            scratch_shapes=[pltpu.VMEM((total, slice_len, width), f32), pltpu.SMEM((total,), jnp.int32)],
            name="align",
        )(owner, block_slot, got)
        aligned = exchange(mean)
        asked = got
    else:
        pieces = sharer_values.reshape(blocks, devices, slice_len * width).transpose(1, 0, 2)
        got = exchange(pieces).reshape(total, slice_len * width)
        dest = owner * blocks + block_slot
        hot = (dest[None, :] == jnp.arange(total, dtype=jnp.int32)[:, None]).astype(bf16)
        sums = jnp.dot(hot, got, preferred_element_type=f32)
        count = jnp.sum(hot.astype(f32), axis=1, keepdims=True)
        mean = (sums / jnp.maximum(count, 1.0)).astype(bf16)
        aligned = exchange(mean.reshape(devices, blocks, slice_len * width))
        aligned = aligned.reshape(devices, blocks, slice_len, width).transpose(1, 0, 2, 3)
        aligned = aligned.reshape(tokens, width)
        asked = lax.all_gather(queries.reshape(1, heads * G, DH), "ctx", axis=0, tiled=True)

    weights, part = pl.pallas_call(
        functools.partial(score_kernel, heads=heads),
        out_shape=(
            shape((heads, rows * G, tokens), bf16),
            shape((rows, heads * G + STAT, DH), f32),
        ),
        in_specs=[SMEM, VMEM, VMEM, VMEM, VMEM],
        cost_estimate=pl.CostEstimate(
            flops=2 * heads * rows * G * tokens * DH,
            bytes_accessed=2 * 10**6,
            transcendentals=heads * rows * G * tokens,
        ),
        name="score",
    )(place, asked, recv_keys, new_keys, new_values)
    merged, numer = pl.pallas_call(
        functools.partial(
            mixer_kernel, blocks=blocks, slice_len=slice_len if tiled else 0, chunk=512
        ),
        out_shape=(shape((tokens, width), bf16), shape(part.shape, f32)),
        in_specs=[SMEM] + [VMEM] * 7,
        name="mixer",
    )(gate_logit, aligned, recv_values, mixer_gate, mixer_up, mixer_down, weights, part)
    attended = pl.pallas_call(
        functools.partial(combine_kernel, heads=heads),
        out_shape=shape((1, heads * G * DH), bf16),
        scratch_shapes=[pltpu.VMEM((heads * G, DH), f32)],
        name="combine",
    )(exchange(numer))
    return merged, attended


def solution(mesh):
    rows = P(("grp", "ctx"), "head")
    return jax.shard_map(
        body,
        mesh=mesh,
        in_specs=(P("grp", None), P("grp"), rows, rows, rows, rows, rows, rows, P(), P(), P(), P("head")),
        out_specs=(rows, rows),
        check_vma=False,
    )
```

time: 280 us -> 56.4 us (0.20)
  blocking collectives: 159 us -> 29.9 us
  waiting for transfers between devices: 67.2 us -> 6.3 us
  matrix products: 16.2 us -> 0 us
  Pallas kernels: 0 us -> 15 us
  between operations: 14.2 us -> 0.65 us
  local copies, waits for them, and re-layouts: 9.63 us -> 0.69 us
  starting transfers between devices: 10.9 us -> 3.41 us
    all_gather x3 -> x0, blocking collectives: 84.6 us -> none  [the longest x1 32 us: body(): lax.all_gather(queries, 'ctx', axis=0, tiled=True)]
    psum x1 -> x0, waiting for transfers between devices: 67.2 us -> none  [body(): numer_all, denom_all = lax.psum((numer_part, denom_part), 'ctx')]
    psum x1 -> x0, blocking collectives: 37.6 us -> none  [body(): numer_all, denom_all = lax.psum((numer_part, denom_part), 'ctx')]
    pmax x1 -> x0, blocking collectives: 36.4 us -> none  [body(): cache_top = lax.pmax(jnp.max(scores, axis=3), 'ctx')]
    all_to_all x0 -> x2, blocking collectives: none -> 29.9 us  [exchange(): return lax.all_to_all(x, 'ctx', split_axis=0, concat_axis=0, tiled=True)]
    dot_general x10 -> x0, matrix products: 16.2 us -> none  [the longest x2 7.73 us: mixer_block(): jnp.dot(hidden, mixer_down, preferred_element_type=jnp.float32)]
    pallas_call x0 -> x5, Pallas kernels: none -> 15 us  [the longest x1 7.6 us: body(): pl.pallas_call(functools.partial(mixer_kernel, blocks=blocks, slice_len=s...]
    all_to_all x2 -> x1, starting transfers between devices: 10.8 us -> 3.41 us  [exchange(): return lax.all_to_all(x, 'ctx', split_axis=0, concat_axis=0, tiled=True)]
  transfers between devices with their start and end apart: 3 -> 1, of which waited for: 1 -> 1; matrix products, arithmetic and copies ran while one was open for 2% -> 0% of each run, Pallas kernels for 0% -> 4%
where the time goes in v1:
time: 56.4 us; the launch traced here: 55.9 us
  blocking collectives  29.9 us (53%)
  Pallas kernels  15 us (27%)
  waiting for transfers between devices  6.3 us (11%)
  starting transfers between devices  3.41 us (6%)
  local copies, waits for them, and re-layouts  0.69 us (1%)
  between operations  0.65 us (1%)
    all_to_all x2, blocking collectives, exchange(): return lax.all_to_all(x, 'ctx', split_axis=0, concat_axis=0, tiled=True)  29.9 us
    pallas_call x1, Pallas kernels, body(): pl.pallas_call(functools.partial(mixer_kernel, blocks=blocks, slice_len=s...  7.6 us
    all_to_all x1, waiting for transfers between devices, exchange(): return lax.all_to_all(x, 'ctx', split_axis=0, concat_axis=0, tiled=True)  6.3 us
    all_to_all x1, starting transfers between devices, exchange(): return lax.all_to_all(x, 'ctx', split_axis=0, concat_axis=0, tiled=True)  3.41 us
    pallas_call x1, Pallas kernels, body(): pl.pallas_call(functools.partial(score_kernel, heads=heads), out_shape=(s...  2.14 us
    pallas_call x1, Pallas kernels, body(): pl.pallas_call(functools.partial(align_kernel, blocks=blocks, slice_len=s...  1.85 us
    pallas_call x1, Pallas kernels, body(): pl.pallas_call(functools.partial(pack_kernel, blocks=blocks, slice_len=sl...  1.72 us
    pallas_call x1, Pallas kernels, body(): pl.pallas_call(functools.partial(combine_kernel, heads=heads), out_shape=...  1.68 us
  transfers between devices with their start and end apart: 1, of which 1 were waited for; matrix products, arithmetic and copies ran while one was open for 0% of the time, Pallas kernels for 4%

profile of v1, /device:TPU:0, one launch (start us, length us, event | category | flops | bytes accessed | tf_op | source)
XLA Modules:
  0.0 55.9 jit_solution(14031748875095835161)
XLA Ops:
  0.6 1.7 %pack.1 = bf16[8,32,640]{2,1,0:T(8,128)(2,1)} custom-call(bf16[256,512]{1,0:T(8,128)(2,1)} %sharer_ref.1, bf16[1,4096]{1,0:T(2,128)(2,1)} %query_ref.1), custom_call_target="tpu_custom_call" | custom-call | tf_op jit(solution)/shard_map/pack/pallas_call | solution.py:180
  2.4 18.3 %all_to_all.15.got_ref = bf16[8,32,640]{2,1,0:T(8,128)(2,1)} all-to-all(bf16[8,32,640]{2,1,0:T(8,128)(2,1)} %pack.1), channel_id=1, replica_groups=mesh['grp'=2,'ctx'=8,'head'=2] {'ctx'}, dimensions={0} | all-to-all | bytes 655360 | tf_op jit(solution)/shard_map/all_to_all | solution.py:21
  20.6 1.9 %align.1 = bf16[8,32,512]{2,1,0:T(8,128)(2,1)} custom-call(s32[16]{0:T(128)} %bitcast.2, s32[16]{0:T(128)} %slot_ref.1, bf16[8,32,640]{2,1,0:T(8,128)(2,1)} %all_to_all.15.got_ref), custom_call_target="tpu_custom_call" | custom-call | tf_op jit(solution)/shard_map/align/pallas_call | solution.py:187
  22.5 3.4 %all-to-all-start.1 = ((bf16[8,32,512]{2,1,0:T(8,128)(2,1)}), bf16[8,32,512]{2,1,0:T(8,128)(2,1)S(1)}, u32[]{:S(2)}, u32[]{:S(2)}) async-start(bf16[8,32,512]{2,1,0:T(8,128)(2,1)} %align.1), calls=%async_computation.1 | async-start | bytes 524288 | tf_op jit(solution)/shard_map/all_to_all | solution.py:21
  25.9 2.1 %score.1 = (bf16[4,64,256]{2,1,0:T(8,128)(2,1)}, f32[8,40,128]{2,1,0:T(8,128)}) custom-call(s32[1]{0:T(128)} %bitcast.1.place_ref, bf16[8,32,640]{2,1,0:T(8,128)(2,1)} %all_to_all.15.got_ref, bf16[256,512]{1,0:T(8,128)(2,1)} %key_ref.1, bf16[1,512]{1,0:T(2,128)(2,1)} %new_key_ref.1, bf16[1,512]{1,0:T(2,128)(2,1)} %new_value_ref.1), custom_call_target="tpu_custom_call" | custom-call | flops 16777216 | bytes 2000000 | tf_op jit(solution)/shard_map/score/pallas_call | solution.py:209
  28.1 6.3 %all-to-all-done.1.got_ref = bf16[8,32,512]{2,1,0:T(8,128)(2,1)S(1)} async-done(((bf16[8,32,512]{2,1,0:T(8,128)(2,1)}), bf16[8,32,512]{2,1,0:T(8,128)(2,1)S(1)}, u32[]{:S(2)}, u32[]{:S(2)}) %all-to-all-start.1) | async-done | bytes 262176 | tf_op jit(solution)/shard_map/all_to_all | solution.py:21
  34.4 0.0 copy-start
  34.4 0.7 %copy-done = bf16[8,32,512]{2,1,0:T(8,128)(2,1)} copy-done((bf16[8,32,512]{2,1,0:T(8,128)(2,1)}, bf16[8,32,512]{2,1,0:T(8,128)(2,1)S(1)}, u32[]{:S(2)}) %copy-start) | copy-done | bytes 262168
  35.1 7.6 %mixer.1 = (bf16[256,512]{1,0:T(8,128)(2,1)}, f32[8,40,128]{2,1,0:T(8,128)}) custom-call(f32[4]{0:T(128)} %logit_ref.1, bf16[8,32,512]{2,1,0:T(8,128)(2,1)} %copy-done, bf16[256,512]{1,0:T(8,128)(2,1)} %value_ref.1, bf16[256,2048]{1,0:T(8,128)(2,1)} %gate_ref.1, bf16[256,2048]{1,0:T(8,128)(2,1)} %up_ref.1, bf16[2048,128]{1,0:T(8,128)(2,1)} %down_ref.1, ...), custom_call_target="tpu_custom_call" | custom-call | tf_op jit(solution)/shard_map/mixer/pallas_call | solution.py:223
  42.7 11.6 %all_to_all.16.got_ref = f32[8,40,128]{2,1,0:T(8,128)} all-to-all(f32[8,40,128]{2,1,0:T(8,128)} %get-tuple-element.9), channel_id=1, replica_groups=mesh['grp'=2,'ctx'=8,'head'=2] {'ctx'}, dimensions={0} | all-to-all | bytes 327680 | tf_op jit(solution)/shard_map/all_to_all | solution.py:21
  54.2 1.7 %combine.1 = bf16[1,4096]{1,0:T(2,128)(2,1)} custom-call(f32[8,40,128]{2,1,0:T(8,128)} %all_to_all.16.got_ref), custom_call_target="tpu_custom_call" | custom-call | tf_op jit(solution)/shard_map/combine/pallas_call | solution.py:231
Async XLA Ops:
  22.5 11.9 %all-to-all-start.1 = ((bf16[8,32,512]{2,1,0:T(8,128)(2,1)}), bf16[8,32,512]{2,1,0:T(8,128)(2,1)S(1)}, u32[]{:S(2)}, u32[]{:S(2)}) async-start(bf16[8,32,512]{2,1,0:T(8,128)(2,1)} %align.1), calls=%async_computation.1 | async-start | bytes 524288 | tf_op jit(solution)/shard_map/all_to_all | solution.py:21
  34.4 0.7 %copy-start = (bf16[8,32,512]{2,1,0:T(8,128)(2,1)}, bf16[8,32,512]{2,1,0:T(8,128)(2,1)S(1)}, u32[]{:S(2)}) copy-start(bf16[8,32,512]{2,1,0:T(8,128)(2,1)S(1)} %all-to-all-done.1.got_ref) | copy-start | bytes 786436

commit v2 on v1

--- a/solution.py
+++ b/solution.py
@@ -15,6 +15,7 @@
 NEG = -1e30
 SMEM = pl.BlockSpec(memory_space=pltpu.SMEM)
 VMEM = pl.BlockSpec(memory_space=pltpu.VMEM)
+ANY = pl.BlockSpec(memory_space=pl.ANY)
 
 
 def exchange(x):
@@ -58,7 +59,14 @@
         out_ref[d, k * slice_len : (k + 1) * slice_len, :] = (sums[r] / many).astype(jnp.bfloat16)
 
 
-def score_kernel(place_ref, got_ref, key_ref, new_key_ref, new_value_ref, weight_ref, part_ref, *, heads):
+def score_kernel(
+    place_ref, got_ref, key_ref, new_key_ref, new_value_ref, gate_hbm, up_hbm, down_hbm,
+    weight_ref, part_ref, gate_ref, up_ref, down_ref, sems, *, heads
+):
+    pairs = ((gate_hbm, gate_ref), (up_hbm, up_ref), (down_hbm, down_ref))
+    copies = [pltpu.make_async_copy(a, b, sems.at[i]) for i, (a, b) in enumerate(pairs)]
+    for copy in copies:
+        copy.start()
     rows = got_ref.shape[0]
     scale = 1.0 / math.sqrt(DH)
     q_all = got_ref[:, :, got_ref.shape[2] - DH :].astype(jnp.float32)
@@ -103,41 +111,46 @@
     part_ref[:, heads * G :, :] = jnp.where(
         sub == 0, jnp.broadcast_to(tops, (rows, STAT, DH)), jnp.broadcast_to(dens, (rows, STAT, DH))
     )
+    for copy in copies:
+        copy.wait()
 
 
 def mixer_kernel(
     logit_ref, got_ref, value_ref, gate_ref, up_ref, down_ref, weight_ref, part_ref, merged_ref, out_ref,
-    *, blocks, slice_len, chunk
+    *, blocks, slice_len
 ):
     tokens, width = value_ref.shape
     heads = width // DH
-    hidden = gate_ref.shape[1]
     rows = part_ref.shape[0]
     out_ref[:, heads * G :, :] = part_ref[:, heads * G :, :]
+    updates = []
+    for first in range(0, heads, 2):
+        joined = []
+        for j in range(first, first + 2):
+            cols = slice(j * DH, (j + 1) * DH)
+            if slice_len:
+                a = jnp.concatenate(
+                    [
+                        got_ref[s, k * slice_len : (k + 1) * slice_len, cols]
+                        for k in range(blocks)
+                        for s in range(got_ref.shape[0])
+                    ],
+                    axis=0,
+                )
+            else:
+                a = got_ref[:, cols]
+            joined.append(jnp.concatenate([value_ref[:, cols], a], axis=1))
+        x = jnp.concatenate(joined, axis=0)
+        g = jnp.dot(x, gate_ref[...], preferred_element_type=jnp.float32)
+        u = jnp.dot(x, up_ref[...], preferred_element_type=jnp.float32)
+        half = g * 0.5
+        h = ((half + half * jnp.tanh(half)) * u).astype(jnp.bfloat16)
+        updates.append(jnp.dot(h, down_ref[...], preferred_element_type=jnp.float32))
     for j in range(heads):
         cols = slice(j * DH, (j + 1) * DH)
-        v = value_ref[:, cols]
-        if slice_len:
-            a = jnp.concatenate(
-                [
-                    got_ref[s, k * slice_len : (k + 1) * slice_len, cols]
-                    for k in range(blocks)
-                    for s in range(got_ref.shape[0])
-                ],
-                axis=0,
-            )
-        else:
-            a = got_ref[:, cols]
-        x = jnp.concatenate([v, a], axis=1)
-        update = jnp.zeros((tokens, DH), jnp.float32)
-        for c in range(0, hidden, chunk):
-            g = jnp.dot(x, gate_ref[:, c : c + chunk], preferred_element_type=jnp.float32)
-            u = jnp.dot(x, up_ref[:, c : c + chunk], preferred_element_type=jnp.float32)
-            half = g * 0.5
-            h = ((half + half * jnp.tanh(half)) * u).astype(jnp.bfloat16)
-            update += jnp.dot(h, down_ref[c : c + chunk, :], preferred_element_type=jnp.float32)
+        update = updates[j // 2][(j % 2) * tokens : (j % 2 + 1) * tokens]
         head_gate = jax.nn.sigmoid(jnp.full((1, DH), logit_ref[j], jnp.float32))
-        merged = (v.astype(jnp.float32) + head_gate * update).astype(jnp.bfloat16)
+        merged = (value_ref[:, cols].astype(jnp.float32) + head_gate * update).astype(jnp.bfloat16)
         merged_ref[:, cols] = merged
         numer = jnp.dot(weight_ref[j], merged, preferred_element_type=jnp.float32)
         out_ref[:, j * G : (j + 1) * G, :] = part_ref[:, j * G : (j + 1) * G, :] + numer.reshape(
@@ -175,6 +188,10 @@
     tiled = slice_len % 16 == 0
     f32, bf16 = jnp.float32, jnp.bfloat16
     shape = jax.ShapeDtypeStruct
+    near = pltpu.VMEM if tiled else shape
+
+    def here(x):
+        return pltpu.with_memory_space_constraint(x, pltpu.VMEM) if tiled else x
 
     if tiled:
         send = pl.pallas_call(
@@ -183,7 +200,7 @@
             scratch_shapes=[pltpu.VMEM((heads * G, DH), f32)],
             name="pack",
         )(sharer_values, queries)
-        got = exchange(send)
+        got = here(exchange(send))
         mean = pl.pallas_call(
             functools.partial(align_kernel, blocks=blocks, slice_len=slice_len),
             out_shape=shape((devices, blocks * slice_len, width), bf16),
@@ -206,34 +223,41 @@
         aligned = aligned.reshape(tokens, width)
         asked = lax.all_gather(queries.reshape(1, heads * G, DH), "ctx", axis=0, tiled=True)
 
-    weights, part = pl.pallas_call(
+    weights, part, gate_v, up_v, down_v = pl.pallas_call(
         functools.partial(score_kernel, heads=heads),
         out_shape=(
             shape((heads, rows * G, tokens), bf16),
             shape((rows, heads * G + STAT, DH), f32),
+            near(mixer_gate.shape, bf16),
+            near(mixer_up.shape, bf16),
+            near(mixer_down.shape, bf16),
         ),
-        in_specs=[SMEM, VMEM, VMEM, VMEM, VMEM],
+        in_specs=[SMEM] + [VMEM] * 4 + [ANY] * 3,
+        scratch_shapes=[pltpu.SemaphoreType.DMA((3,))],
         cost_estimate=pl.CostEstimate(
             flops=2 * heads * rows * G * tokens * DH,
             bytes_accessed=2 * 10**6,
             transcendentals=heads * rows * G * tokens,
         ),
         name="score",
-    )(place, asked, recv_keys, new_keys, new_values)
+    )(
+        place, asked, recv_keys, new_keys, new_values, mixer_gate, mixer_up, mixer_down
+    )
     merged, numer = pl.pallas_call(
-        functools.partial(
-            mixer_kernel, blocks=blocks, slice_len=slice_len if tiled else 0, chunk=512
-        ),
+        functools.partial(mixer_kernel, blocks=blocks, slice_len=slice_len if tiled else 0),
         out_shape=(shape((tokens, width), bf16), shape(part.shape, f32)),
         in_specs=[SMEM] + [VMEM] * 7,
         name="mixer",
-    )(gate_logit, aligned, recv_values, mixer_gate, mixer_up, mixer_down, weights, part)
+    )(
+        gate_logit, here(aligned), recv_values, here(gate_v), here(up_v), here(down_v),
+        weights, part,
+    )
     attended = pl.pallas_call(
         functools.partial(combine_kernel, heads=heads),
         out_shape=shape((1, heads * G * DH), bf16),
         scratch_shapes=[pltpu.VMEM((heads * G, DH), f32)],
         name="combine",
-    )(exchange(numer))
+    )(here(exchange(numer)))
     return merged, attended
 
 

time: 56.4 us -> 52.2 us (0.926)
  Pallas kernels: 15 us -> 13.3 us
  waiting for transfers between devices: 6.3 us -> 5.05 us
  local copies, waits for them, and re-layouts: 0.69 us -> 0 us
  blocking collectives: 29.9 us -> 29.3 us
    pallas_call x1, Pallas kernels: 7.6 us -> 5.86 us  [body(): pl.pallas_call(functools.partial(mixer_kernel, blocks=blocks, slice_len=s...]
    all_to_all x1, waiting for transfers between devices: 6.3 us -> 5.05 us  [exchange(): return lax.all_to_all(x, 'ctx', split_axis=0, concat_axis=0, tiled=True)]
    pallas_call x1, Pallas kernels: 2.14 us -> 3.38 us  [body(): pl.pallas_call(functools.partial(score_kernel, heads=heads), out_shape=(s...]
    pallas_call x1, Pallas kernels: 1.68 us -> 0.76 us  [body(): pl.pallas_call(functools.partial(combine_kernel, heads=heads), out_shape=...]
    unnamed x2 -> x0, local copies, waits for them, and re-layouts: 0.69 us -> none
    all_to_all x2, blocking collectives: 29.9 us -> 29.3 us  [exchange(): return lax.all_to_all(x, 'ctx', split_axis=0, concat_axis=0, tiled=True)]
  transfers between devices with their start and end apart: 1 -> 1, of which waited for: 1 -> 1; matrix products, arithmetic and copies ran while one was open for 0% -> 0% of each run, Pallas kernels for 4% -> 7%
where the time goes in v2:
time: 52.2 us; the launch traced here: 51.6 us
  blocking collectives  29.3 us (56%)
  Pallas kernels  13.3 us (25%)
  waiting for transfers between devices  5.05 us (10%)
  starting transfers between devices  3.41 us (7%)
  between operations  0.65 us (1%)
    all_to_all x2, blocking collectives, exchange(): return lax.all_to_all(x, 'ctx', split_axis=0, concat_axis=0, tiled=True)  29.3 us
    pallas_call x1, Pallas kernels, body(): pl.pallas_call(functools.partial(mixer_kernel, blocks=blocks, slice_len=s...  5.86 us
    all_to_all x1, waiting for transfers between devices, exchange(): return lax.all_to_all(x, 'ctx', split_axis=0, concat_axis=0, tiled=True)  5.05 us
    all_to_all x1, starting transfers between devices, exchange(): return lax.all_to_all(x, 'ctx', split_axis=0, concat_axis=0, tiled=True)  3.41 us
    pallas_call x1, Pallas kernels, body(): pl.pallas_call(functools.partial(score_kernel, heads=heads), out_shape=(s...  3.38 us
    pallas_call x1, Pallas kernels, body(): pl.pallas_call(functools.partial(pack_kernel, blocks=blocks, slice_len=sl...  1.71 us
    pallas_call x1, Pallas kernels, body(): pl.pallas_call(functools.partial(align_kernel, blocks=blocks, slice_len=s...  1.54 us
  transfers between devices with their start and end apart: 1, of which 1 were waited for; matrix products, arithmetic and copies ran while one was open for 0% of the time, Pallas kernels for 7%

profile of v2, /device:TPU:0, one launch (start us, length us, event | category | flops | bytes accessed | tf_op | source)
XLA Modules:
  0.0 51.6 jit_solution(18066385851566004341)
XLA Ops:
  0.6 1.7 %pack.1 = bf16[8,32,640]{2,1,0:T(8,128)(2,1)} custom-call(bf16[256,512]{1,0:T(8,128)(2,1)} %sharer_ref.1, bf16[1,4096]{1,0:T(2,128)(2,1)} %query_ref.1), custom_call_target="tpu_custom_call" | custom-call | tf_op jit(solution)/shard_map/pack/pallas_call | solution.py:197
  2.3 18.2 %all_to_all.15.got_ref = bf16[8,32,640]{2,1,0:T(8,128)(2,1)S(1)} all-to-all(bf16[8,32,640]{2,1,0:T(8,128)(2,1)} %pack.1), channel_id=1, replica_groups=mesh['grp'=2,'ctx'=8,'head'=2] {'ctx'}, dimensions={0} | all-to-all | bytes 655360 | tf_op jit(solution)/shard_map/all_to_all | solution.py:22
  20.5 1.5 %align.1 = bf16[8,32,512]{2,1,0:T(8,128)(2,1)} custom-call(s32[16]{0:T(128)} %bitcast.2, s32[16]{0:T(128)} %slot_ref.1, bf16[8,32,640]{2,1,0:T(8,128)(2,1)S(1)} %all_to_all.15.got_ref), custom_call_target="tpu_custom_call" | custom-call | tf_op jit(solution)/shard_map/align/pallas_call | solution.py:204
  22.1 3.4 %all-to-all-start.1 = ((bf16[8,32,512]{2,1,0:T(8,128)(2,1)}), bf16[8,32,512]{2,1,0:T(8,128)(2,1)S(1)}, u32[]{:S(2)}, u32[]{:S(2)}) async-start(bf16[8,32,512]{2,1,0:T(8,128)(2,1)} %align.1), calls=%async_computation.1 | async-start | bytes 524288 | tf_op jit(solution)/shard_map/all_to_all | solution.py:22
  25.5 3.4 %score.1 = (bf16[4,64,256]{2,1,0:T(8,128)(2,1)}, f32[8,40,128]{2,1,0:T(8,128)}, bf16[256,2048]{1,0:T(8,128)(2,1)S(1)}, bf16[256,2048]{1,0:T(8,128)(2,1)S(1)}, bf16[2048,128]{1,0:T(8,128)(2,1)S(1)}) custom-call(s32[1]{0:T(128)} %bitcast.1.place_ref, bf16[8,32,640]{2,1,0:T(8,128)(2,1)S(1)} %all_to_all.15.got_ref, bf16[256,512]{1,0:T(8,128)(2,1)} %key_ref.1, ...), custom_call_target="tpu_custom_call" | custom-call | flops 16777216 | bytes 2000000 | tf_op jit(solution)/shard_map/score/pallas_call | solution.py:226
  28.9 5.0 %all-to-all-done.1.got_ref = bf16[8,32,512]{2,1,0:T(8,128)(2,1)S(1)} async-done(((bf16[8,32,512]{2,1,0:T(8,128)(2,1)}), bf16[8,32,512]{2,1,0:T(8,128)(2,1)S(1)}, u32[]{:S(2)}, u32[]{:S(2)}) %all-to-all-start.1) | async-done | bytes 262176 | tf_op jit(solution)/shard_map/all_to_all | solution.py:22
  33.9 5.9 %mixer.1 = (bf16[256,512]{1,0:T(8,128)(2,1)}, f32[8,40,128]{2,1,0:T(8,128)}) custom-call(f32[4]{0:T(128)} %logit_ref.1, bf16[8,32,512]{2,1,0:T(8,128)(2,1)S(1)} %all-to-all-done.1.got_ref, bf16[256,512]{1,0:T(8,128)(2,1)} %value_ref.1, bf16[256,2048]{1,0:T(8,128)(2,1)S(1)} %get-tuple-element.9.gate_ref, bf16[256,2048]{1,0:T(8,128)(2,1)S(1)} %get-tuple-element.10.up_ref, ...), custom_call_target="tpu_custom_call" | custom-call | tf_op jit(solution)/shard_map/mixer/pallas_call | solution.py:246
  39.8 11.1 %all_to_all.16.got_ref = f32[8,40,128]{2,1,0:T(8,128)S(1)} all-to-all(f32[8,40,128]{2,1,0:T(8,128)} %get-tuple-element.15), channel_id=1, replica_groups=mesh['grp'=2,'ctx'=8,'head'=2] {'ctx'}, dimensions={0} | all-to-all | bytes 327680 | tf_op jit(solution)/shard_map/all_to_all | solution.py:22
  50.9 0.8 %combine.1 = bf16[1,4096]{1,0:T(2,128)(2,1)} custom-call(f32[8,40,128]{2,1,0:T(8,128)S(1)} %all_to_all.16.got_ref), custom_call_target="tpu_custom_call" | custom-call | tf_op jit(solution)/shard_map/combine/pallas_call | solution.py:255
Async XLA Ops:
  22.1 11.9 %all-to-all-start.1 = ((bf16[8,32,512]{2,1,0:T(8,128)(2,1)}), bf16[8,32,512]{2,1,0:T(8,128)(2,1)S(1)}, u32[]{:S(2)}, u32[]{:S(2)}) async-start(bf16[8,32,512]{2,1,0:T(8,128)(2,1)} %align.1), calls=%async_computation.1 | async-start | bytes 524288 | tf_op jit(solution)/shard_map/all_to_all | solution.py:22

commit v3 on v2

--- a/solution.py
+++ b/solution.py
@@ -28,17 +28,25 @@
     return scratch[...].astype(jnp.bfloat16)
 
 
-def pack_kernel(sharer_ref, query_ref, out_ref, scratch, *, blocks, slice_len):
+def pack_kernel(sharer_hbm, query_ref, out_ref, scratch, sems, *, blocks, slice_len):
     devices = out_ref.shape[0]
-    width = sharer_ref.shape[1]
+    width = sharer_hbm.shape[1]
+    copies = []
+    for d in range(devices):
+        for k in range(blocks):
+            copies.append(
+                pltpu.make_async_copy(
+                    sharer_hbm.at[pl.ds(k * BLK + d * slice_len, slice_len), :],
+                    out_ref.at[d, pl.ds(k * slice_len, slice_len), pl.ds(0, width)],
+                    sems.at[d, k],
+                )
+            )
+            copies[-1].start()
     q = query_tile(query_ref, scratch)
     for d in range(devices):
-        for k in range(blocks):
-            start = k * BLK + d * slice_len
-            out_ref[d, k * slice_len : (k + 1) * slice_len, :width] = sharer_ref[
-                start : start + slice_len, :
-            ]
         out_ref[d, :, width:] = q
+    for copy in copies:
+        copy.wait()
 
 
 def align_kernel(owner_ref, slot_ref, got_ref, out_ref, sums, counts, *, blocks, slice_len):
@@ -196,14 +204,18 @@
     if tiled:
         send = pl.pallas_call(
             functools.partial(pack_kernel, blocks=blocks, slice_len=slice_len),
-            out_shape=shape((devices, blocks * slice_len, width + DH), bf16),
-            scratch_shapes=[pltpu.VMEM((heads * G, DH), f32)],
+            out_shape=near((devices, blocks * slice_len, width + DH), bf16),
+            in_specs=[ANY, VMEM],
+            scratch_shapes=[
+                pltpu.VMEM((heads * G, DH), f32),
+                pltpu.SemaphoreType.DMA((devices, blocks)),
+            ],
             name="pack",
         )(sharer_values, queries)
         got = here(exchange(send))
         mean = pl.pallas_call(
             functools.partial(align_kernel, blocks=blocks, slice_len=slice_len),
-            out_shape=shape((devices, blocks * slice_len, width), bf16),
+            out_shape=near((devices, blocks * slice_len, width), bf16),
             in_specs=[SMEM, SMEM, VMEM],
             scratch_shapes=[pltpu.VMEM((total, slice_len, width), f32), pltpu.SMEM((total,), jnp.int32)],
             name="align",
@@ -245,7 +257,7 @@
     )
     merged, numer = pl.pallas_call(
         functools.partial(mixer_kernel, blocks=blocks, slice_len=slice_len if tiled else 0),
-        out_shape=(shape((tokens, width), bf16), shape(part.shape, f32)),
+        out_shape=(shape((tokens, width), bf16), near(part.shape, f32)),
         in_specs=[SMEM] + [VMEM] * 7,
         name="mixer",
     )(

time: 52.2 us -> 51.7 us (level)
  no operation moved by 1% of the time
where the time goes in v3:
time: 51.7 us; the launch traced here: 51.2 us
  blocking collectives  28.9 us (56%)
  Pallas kernels  13.2 us (26%)
  waiting for transfers between devices  5.04 us (10%)
  starting transfers between devices  3.41 us (7%)
  between operations  0.66 us (1%)
    all_to_all x2, blocking collectives, exchange(): return lax.all_to_all(x, 'ctx', split_axis=0, concat_axis=0, tiled=True)  28.9 us
    pallas_call x1, Pallas kernels, body(): pl.pallas_call(functools.partial(mixer_kernel, blocks=blocks, slice_len=s...  5.77 us
    all_to_all x1, waiting for transfers between devices, exchange(): return lax.all_to_all(x, 'ctx', split_axis=0, concat_axis=0, tiled=True)  5.04 us
    all_to_all x1, starting transfers between devices, exchange(): return lax.all_to_all(x, 'ctx', split_axis=0, concat_axis=0, tiled=True)  3.41 us
    pallas_call x1, Pallas kernels, body(): pl.pallas_call(functools.partial(score_kernel, heads=heads), out_shape=(s...  3.39 us
    pallas_call x1, Pallas kernels, body(): pl.pallas_call(functools.partial(pack_kernel, blocks=blocks, slice_len=sl...  1.76 us
    pallas_call x1, Pallas kernels, body(): pl.pallas_call(functools.partial(align_kernel, blocks=blocks, slice_len=s...  1.54 us
  transfers between devices with their start and end apart: 1, of which 1 were waited for; matrix products, arithmetic and copies ran while one was open for 0% of the time, Pallas kernels for 7%

profile of v3, /device:TPU:0, one launch (start us, length us, event | category | flops | bytes accessed | tf_op | source)
XLA Modules:
  0.0 51.2 jit_solution(209520416890985571)
XLA Ops:
  0.6 1.8 %pack.1 = bf16[8,32,640]{2,1,0:T(8,128)(2,1)S(1)} custom-call(bf16[256,512]{1,0:T(8,128)(2,1)} %sharer_hbm.1, bf16[1,4096]{1,0:T(2,128)(2,1)} %query_ref.1), custom_call_target="tpu_custom_call" | custom-call | tf_op jit(solution)/shard_map/pack/pallas_call | solution.py:205
  2.4 18.0 %all_to_all.15.got_ref = bf16[8,32,640]{2,1,0:T(8,128)(2,1)S(1)} all-to-all(bf16[8,32,640]{2,1,0:T(8,128)(2,1)S(1)} %pack.1), channel_id=1, replica_groups=mesh['grp'=2,'ctx'=8,'head'=2] {'ctx'}, dimensions={0} | all-to-all | bytes 655360 | tf_op jit(solution)/shard_map/all_to_all | solution.py:22
  20.4 1.5 %align.1 = bf16[8,32,512]{2,1,0:T(8,128)(2,1)} custom-call(s32[16]{0:T(128)} %bitcast.2, s32[16]{0:T(128)} %slot_ref.1, bf16[8,32,640]{2,1,0:T(8,128)(2,1)S(1)} %all_to_all.15.got_ref), custom_call_target="tpu_custom_call" | custom-call | tf_op jit(solution)/shard_map/align/pallas_call | solution.py:216
  21.9 3.4 %all-to-all-start.1 = ((bf16[8,32,512]{2,1,0:T(8,128)(2,1)}), bf16[8,32,512]{2,1,0:T(8,128)(2,1)S(1)}, u32[]{:S(2)}, u32[]{:S(2)}) async-start(bf16[8,32,512]{2,1,0:T(8,128)(2,1)} %align.1), calls=%async_computation.1 | async-start | bytes 524288 | tf_op jit(solution)/shard_map/all_to_all | solution.py:22
  25.4 3.4 %score.1 = (bf16[4,64,256]{2,1,0:T(8,128)(2,1)}, f32[8,40,128]{2,1,0:T(8,128)}, bf16[256,2048]{1,0:T(8,128)(2,1)S(1)}, bf16[256,2048]{1,0:T(8,128)(2,1)S(1)}, bf16[2048,128]{1,0:T(8,128)(2,1)S(1)}) custom-call(s32[1]{0:T(128)} %bitcast.1.place_ref, bf16[8,32,640]{2,1,0:T(8,128)(2,1)S(1)} %all_to_all.15.got_ref, bf16[256,512]{1,0:T(8,128)(2,1)} %key_ref.1, ...), custom_call_target="tpu_custom_call" | custom-call | flops 16777216 | bytes 2000000 | tf_op jit(solution)/shard_map/score/pallas_call | solution.py:238
  28.8 5.0 %all-to-all-done.1.got_ref = bf16[8,32,512]{2,1,0:T(8,128)(2,1)S(1)} async-done(((bf16[8,32,512]{2,1,0:T(8,128)(2,1)}), bf16[8,32,512]{2,1,0:T(8,128)(2,1)S(1)}, u32[]{:S(2)}, u32[]{:S(2)}) %all-to-all-start.1) | async-done | bytes 262176 | tf_op jit(solution)/shard_map/all_to_all | solution.py:22
  33.8 5.8 %mixer.1 = (bf16[256,512]{1,0:T(8,128)(2,1)}, f32[8,40,128]{2,1,0:T(8,128)S(1)}) custom-call(f32[4]{0:T(128)} %logit_ref.1, bf16[8,32,512]{2,1,0:T(8,128)(2,1)S(1)} %all-to-all-done.1.got_ref, bf16[256,512]{1,0:T(8,128)(2,1)} %value_ref.1, bf16[256,2048]{1,0:T(8,128)(2,1)S(1)} %get-tuple-element.9.gate_ref, bf16[256,2048]{1,0:T(8,128)(2,1)S(1)} %get-tuple-element.10.up_ref, ...), custom_call_target="tpu_custom_call" | custom-call | tf_op jit(solution)/shard_map/mixer/pallas_call | solution.py:258
  39.6 10.9 %all_to_all.16.got_ref = f32[8,40,128]{2,1,0:T(8,128)S(1)} all-to-all(f32[8,40,128]{2,1,0:T(8,128)S(1)} %get-tuple-element.15), channel_id=1, replica_groups=mesh['grp'=2,'ctx'=8,'head'=2] {'ctx'}, dimensions={0} | all-to-all | bytes 327680 | tf_op jit(solution)/shard_map/all_to_all | solution.py:22
  50.4 0.8 %combine.1 = bf16[1,4096]{1,0:T(2,128)(2,1)} custom-call(f32[8,40,128]{2,1,0:T(8,128)S(1)} %all_to_all.16.got_ref), custom_call_target="tpu_custom_call" | custom-call | tf_op jit(solution)/shard_map/combine/pallas_call | solution.py:267
Async XLA Ops:
  21.9 11.9 %all-to-all-start.1 = ((bf16[8,32,512]{2,1,0:T(8,128)(2,1)}), bf16[8,32,512]{2,1,0:T(8,128)(2,1)S(1)}, u32[]{:S(2)}, u32[]{:S(2)}) async-start(bf16[8,32,512]{2,1,0:T(8,128)(2,1)} %align.1), calls=%async_computation.1 | async-start | bytes 524288 | tf_op jit(solution)/shard_map/all_to_all | solution.py:22

commit v4 on v3

--- a/solution.py
+++ b/solution.py
@@ -28,8 +28,10 @@
     return scratch[...].astype(jnp.bfloat16)
 
 
-def pack_kernel(sharer_hbm, query_ref, out_ref, scratch, sems, *, blocks, slice_len):
+def pack_kernel(sharer_hbm, query_hbm, out_ref, query_ref, scratch, sems, query_sem, *, blocks, slice_len):
     devices = out_ref.shape[0]
+    query_copy = pltpu.make_async_copy(query_hbm, query_ref, query_sem)
+    query_copy.start()
     width = sharer_hbm.shape[1]
     copies = []
     for d in range(devices):
@@ -42,6 +44,7 @@
                 )
             )
             copies[-1].start()
+    query_copy.wait()
     q = query_tile(query_ref, scratch)
     for d in range(devices):
         out_ref[d, :, width:] = q
@@ -124,14 +127,14 @@
 
 
 def mixer_kernel(
-    logit_ref, got_ref, value_ref, gate_ref, up_ref, down_ref, weight_ref, part_ref, merged_ref, out_ref,
-    *, blocks, slice_len
+    logit_ref, got_ref, value_ref, gate_ref, up_ref, down_ref, weight_ref, part_ref, merged_hbm, out_ref,
+    merged_ref, sems, *, blocks, slice_len
 ):
     tokens, width = value_ref.shape
     heads = width // DH
     rows = part_ref.shape[0]
     out_ref[:, heads * G :, :] = part_ref[:, heads * G :, :]
-    updates = []
+    copies = []
     for first in range(0, heads, 2):
         joined = []
         for j in range(first, first + 2):
@@ -153,17 +156,24 @@
         u = jnp.dot(x, up_ref[...], preferred_element_type=jnp.float32)
         half = g * 0.5
         h = ((half + half * jnp.tanh(half)) * u).astype(jnp.bfloat16)
-        updates.append(jnp.dot(h, down_ref[...], preferred_element_type=jnp.float32))
-    for j in range(heads):
-        cols = slice(j * DH, (j + 1) * DH)
-        update = updates[j // 2][(j % 2) * tokens : (j % 2 + 1) * tokens]
-        head_gate = jax.nn.sigmoid(jnp.full((1, DH), logit_ref[j], jnp.float32))
-        merged = (value_ref[:, cols].astype(jnp.float32) + head_gate * update).astype(jnp.bfloat16)
-        merged_ref[:, cols] = merged
-        numer = jnp.dot(weight_ref[j], merged, preferred_element_type=jnp.float32)
-        out_ref[:, j * G : (j + 1) * G, :] = part_ref[:, j * G : (j + 1) * G, :] + numer.reshape(
-            rows, G, DH
-        )
+        updates = jnp.dot(h, down_ref[...], preferred_element_type=jnp.float32)
+        for j in range(first, first + 2):
+            cols = slice(j * DH, (j + 1) * DH)
+            update = updates[(j - first) * tokens : (j - first + 1) * tokens]
+            head_gate = jax.nn.sigmoid(jnp.full((1, DH), logit_ref[j], jnp.float32))
+            merged = (value_ref[:, cols].astype(jnp.float32) + head_gate * update).astype(jnp.bfloat16)
+            merged_ref[:, cols] = merged
+            head = pl.ds(j * DH, DH)
+            copies.append(
+                pltpu.make_async_copy(merged_ref.at[:, head], merged_hbm.at[:, head], sems.at[j])
+            )
+            copies[-1].start()
+            numer = jnp.dot(weight_ref[j], merged, preferred_element_type=jnp.float32)
+            out_ref[:, j * G : (j + 1) * G, :] = part_ref[:, j * G : (j + 1) * G, :] + numer.reshape(
+                rows, G, DH
+            )
+    for copy in copies:
+        copy.wait()
 
 
 def combine_kernel(got_ref, out_ref, scratch, *, heads):
@@ -205,10 +215,12 @@
         send = pl.pallas_call(
             functools.partial(pack_kernel, blocks=blocks, slice_len=slice_len),
             out_shape=near((devices, blocks * slice_len, width + DH), bf16),
-            in_specs=[ANY, VMEM],
+            in_specs=[ANY, ANY],
             scratch_shapes=[
+                pltpu.VMEM(queries.shape, bf16),
                 pltpu.VMEM((heads * G, DH), f32),
                 pltpu.SemaphoreType.DMA((devices, blocks)),
+                pltpu.SemaphoreType.DMA(()),
             ],
             name="pack",
         )(sharer_values, queries)
@@ -259,6 +271,11 @@
         functools.partial(mixer_kernel, blocks=blocks, slice_len=slice_len if tiled else 0),
         out_shape=(shape((tokens, width), bf16), near(part.shape, f32)),
         in_specs=[SMEM] + [VMEM] * 7,
+        out_specs=(ANY, VMEM),
+        scratch_shapes=[
+            pltpu.VMEM((tokens, width), bf16),
+            pltpu.SemaphoreType.DMA((heads,)),
+        ],
         name="mixer",
     )(
         gate_logit, here(aligned), recv_values, here(gate_v), here(up_v), here(down_v),

time: 51.7 us -> 51.6 us (level)
    pallas_call x1, Pallas kernels: 1.76 us -> 1.09 us  [body(): pl.pallas_call(functools.partial(pack_kernel, blocks=blocks, slice_len=sl...]
    pallas_call x1, Pallas kernels: 5.77 us -> 6.4 us  [body(): pl.pallas_call(functools.partial(mixer_kernel, blocks=blocks, slice_len=s...]
where the time goes in v4:
time: 51.6 us; the launch traced here: 51.2 us
  blocking collectives  28.9 us (56%)
  Pallas kernels  13.2 us (26%)
  waiting for transfers between devices  5.04 us (10%)
  starting transfers between devices  3.41 us (7%)
  between operations  0.67 us (1%)
    all_to_all x2, blocking collectives, exchange(): return lax.all_to_all(x, 'ctx', split_axis=0, concat_axis=0, tiled=True)  28.9 us
    pallas_call x1, Pallas kernels, body(): pl.pallas_call(functools.partial(mixer_kernel, blocks=blocks, slice_len=s...  6.4 us
    all_to_all x1, waiting for transfers between devices, exchange(): return lax.all_to_all(x, 'ctx', split_axis=0, concat_axis=0, tiled=True)  5.04 us
    all_to_all x1, starting transfers between devices, exchange(): return lax.all_to_all(x, 'ctx', split_axis=0, concat_axis=0, tiled=True)  3.41 us
    pallas_call x1, Pallas kernels, body(): pl.pallas_call(functools.partial(score_kernel, heads=heads), out_shape=(s...  3.39 us
    pallas_call x1, Pallas kernels, body(): pl.pallas_call(functools.partial(align_kernel, blocks=blocks, slice_len=s...  1.54 us
    pallas_call x1, Pallas kernels, body(): pl.pallas_call(functools.partial(pack_kernel, blocks=blocks, slice_len=sl...  1.09 us
  transfers between devices with their start and end apart: 1, of which 1 were waited for; matrix products, arithmetic and copies ran while one was open for 0% of the time, Pallas kernels for 7%

profile of v4, /device:TPU:0, one launch (start us, length us, event | category | flops | bytes accessed | tf_op | source)
XLA Modules:
  0.0 51.2 jit_solution(10235013584524301977)
XLA Ops:
  0.6 1.1 %pack.1 = bf16[8,32,640]{2,1,0:T(8,128)(2,1)S(1)} custom-call(bf16[256,512]{1,0:T(8,128)(2,1)} %sharer_hbm.1, bf16[1,4096]{1,0:T(2,128)(2,1)} %query_hbm.1), custom_call_target="tpu_custom_call" | custom-call | tf_op jit(solution)/shard_map/pack/pallas_call | solution.py:215
  1.7 18.0 %all_to_all.15.got_ref = bf16[8,32,640]{2,1,0:T(8,128)(2,1)S(1)} all-to-all(bf16[8,32,640]{2,1,0:T(8,128)(2,1)S(1)} %pack.1), channel_id=1, replica_groups=mesh['grp'=2,'ctx'=8,'head'=2] {'ctx'}, dimensions={0} | all-to-all | bytes 655360 | tf_op jit(solution)/shard_map/all_to_all | solution.py:22
  19.7 1.5 %align.1 = bf16[8,32,512]{2,1,0:T(8,128)(2,1)} custom-call(s32[16]{0:T(128)} %bitcast.2, s32[16]{0:T(128)} %slot_ref.1, bf16[8,32,640]{2,1,0:T(8,128)(2,1)S(1)} %all_to_all.15.got_ref), custom_call_target="tpu_custom_call" | custom-call | tf_op jit(solution)/shard_map/align/pallas_call | solution.py:228
  21.3 3.4 %all-to-all-start.1 = ((bf16[8,32,512]{2,1,0:T(8,128)(2,1)}), bf16[8,32,512]{2,1,0:T(8,128)(2,1)S(1)}, u32[]{:S(2)}, u32[]{:S(2)}) async-start(bf16[8,32,512]{2,1,0:T(8,128)(2,1)} %align.1), calls=%async_computation.1 | async-start | bytes 524288 | tf_op jit(solution)/shard_map/all_to_all | solution.py:22
  24.7 3.4 %score.1 = (bf16[4,64,256]{2,1,0:T(8,128)(2,1)}, f32[8,40,128]{2,1,0:T(8,128)}, bf16[256,2048]{1,0:T(8,128)(2,1)S(1)}, bf16[256,2048]{1,0:T(8,128)(2,1)S(1)}, bf16[2048,128]{1,0:T(8,128)(2,1)S(1)}) custom-call(s32[1]{0:T(128)} %bitcast.1.place_ref, bf16[8,32,640]{2,1,0:T(8,128)(2,1)S(1)} %all_to_all.15.got_ref, bf16[256,512]{1,0:T(8,128)(2,1)} %key_ref.1, ...), custom_call_target="tpu_custom_call" | custom-call | flops 16777216 | bytes 2000000 | tf_op jit(solution)/shard_map/score/pallas_call | solution.py:250
  28.1 5.0 %all-to-all-done.1.got_ref = bf16[8,32,512]{2,1,0:T(8,128)(2,1)S(1)} async-done(((bf16[8,32,512]{2,1,0:T(8,128)(2,1)}), bf16[8,32,512]{2,1,0:T(8,128)(2,1)S(1)}, u32[]{:S(2)}, u32[]{:S(2)}) %all-to-all-start.1) | async-done | bytes 262176 | tf_op jit(solution)/shard_map/all_to_all | solution.py:22
  33.1 6.4 %mixer.1 = (bf16[256,512]{1,0:T(8,128)(2,1)}, f32[8,40,128]{2,1,0:T(8,128)S(1)}) custom-call(f32[4]{0:T(128)} %logit_ref.1, bf16[8,32,512]{2,1,0:T(8,128)(2,1)S(1)} %all-to-all-done.1.got_ref, bf16[256,512]{1,0:T(8,128)(2,1)} %value_ref.1, bf16[256,2048]{1,0:T(8,128)(2,1)S(1)} %get-tuple-element.9.gate_ref, bf16[256,2048]{1,0:T(8,128)(2,1)S(1)} %get-tuple-element.10.up_ref, ...), custom_call_target="tpu_custom_call" | custom-call | tf_op jit(solution)/shard_map/mixer/pallas_call | solution.py:270
  39.5 10.9 %all_to_all.16.got_ref = f32[8,40,128]{2,1,0:T(8,128)S(1)} all-to-all(f32[8,40,128]{2,1,0:T(8,128)S(1)} %get-tuple-element.15), channel_id=1, replica_groups=mesh['grp'=2,'ctx'=8,'head'=2] {'ctx'}, dimensions={0} | all-to-all | bytes 327680 | tf_op jit(solution)/shard_map/all_to_all | solution.py:22
  50.4 0.8 %combine.1 = bf16[1,4096]{1,0:T(2,128)(2,1)} custom-call(f32[8,40,128]{2,1,0:T(8,128)S(1)} %all_to_all.16.got_ref), custom_call_target="tpu_custom_call" | custom-call | tf_op jit(solution)/shard_map/combine/pallas_call | solution.py:284
Async XLA Ops:
  21.3 11.9 %all-to-all-start.1 = ((bf16[8,32,512]{2,1,0:T(8,128)(2,1)}), bf16[8,32,512]{2,1,0:T(8,128)(2,1)S(1)}, u32[]{:S(2)}, u32[]{:S(2)}) async-start(bf16[8,32,512]{2,1,0:T(8,128)(2,1)} %align.1), calls=%async_computation.1 | async-start | bytes 524288 | tf_op jit(solution)/shard_map/all_to_all | solution.py:22

commit v5 on v3

--- a/solution.py
+++ b/solution.py
@@ -28,8 +28,10 @@
     return scratch[...].astype(jnp.bfloat16)
 
 
-def pack_kernel(sharer_hbm, query_ref, out_ref, scratch, sems, *, blocks, slice_len):
+def pack_kernel(sharer_hbm, query_hbm, out_ref, query_ref, scratch, sems, query_sem, *, blocks, slice_len):
     devices = out_ref.shape[0]
+    query_copy = pltpu.make_async_copy(query_hbm, query_ref, query_sem)
+    query_copy.start()
     width = sharer_hbm.shape[1]
     copies = []
     for d in range(devices):
@@ -42,6 +44,7 @@
                 )
             )
             copies[-1].start()
+    query_copy.wait()
     q = query_tile(query_ref, scratch)
     for d in range(devices):
         out_ref[d, :, width:] = q
@@ -49,7 +52,9 @@
         copy.wait()
 
 
-def align_kernel(owner_ref, slot_ref, got_ref, out_ref, sums, counts, *, blocks, slice_len):
+def align_kernel(
+    owner_ref, slot_ref, got_ref, out_hbm, out_ref, sums, counts, sems, *, blocks, slice_len
+):
     devices = out_ref.shape[0]
     width = out_ref.shape[2]
     total = devices * blocks
@@ -61,10 +66,16 @@
         s, k = divmod(b, blocks)
         sums[dest] += got_ref[s, k * slice_len : (k + 1) * slice_len, :width].astype(jnp.float32)
         counts[dest] = counts[dest] + 1
+    copies = []
     for r in range(total):
         d, k = divmod(r, blocks)
         many = jnp.full((1, width), jnp.maximum(counts[r], 1), jnp.int32).astype(jnp.float32)
         out_ref[d, k * slice_len : (k + 1) * slice_len, :] = (sums[r] / many).astype(jnp.bfloat16)
+        if k == blocks - 1:
+            copies.append(pltpu.make_async_copy(out_ref.at[d], out_hbm.at[d], sems.at[d]))
+            copies[-1].start()
+    for copy in copies:
+        copy.wait()
 
 
 def score_kernel(
@@ -121,44 +132,39 @@
     )
     for copy in copies:
         copy.wait()
+    gate_ref[...] = gate_ref[...] * 0.5
 
 
 def mixer_kernel(
     logit_ref, got_ref, value_ref, gate_ref, up_ref, down_ref, weight_ref, part_ref, merged_ref, out_ref,
     *, blocks, slice_len
 ):
-    tokens, width = value_ref.shape
-    heads = width // DH
+    heads = value_ref.shape[1] // DH
     rows = part_ref.shape[0]
     out_ref[:, heads * G :, :] = part_ref[:, heads * G :, :]
     updates = []
-    for first in range(0, heads, 2):
-        joined = []
-        for j in range(first, first + 2):
-            cols = slice(j * DH, (j + 1) * DH)
-            if slice_len:
-                a = jnp.concatenate(
-                    [
-                        got_ref[s, k * slice_len : (k + 1) * slice_len, cols]
-                        for k in range(blocks)
-                        for s in range(got_ref.shape[0])
-                    ],
-                    axis=0,
-                )
-            else:
-                a = got_ref[:, cols]
-            joined.append(jnp.concatenate([value_ref[:, cols], a], axis=1))
-        x = jnp.concatenate(joined, axis=0)
-        g = jnp.dot(x, gate_ref[...], preferred_element_type=jnp.float32)
+    for j in range(heads):
+        cols = slice(j * DH, (j + 1) * DH)
+        if slice_len:
+            a = jnp.concatenate(
+                [
+                    got_ref[s, k * slice_len : (k + 1) * slice_len, cols]
+                    for k in range(blocks)
+                    for s in range(got_ref.shape[0])
+                ],
+                axis=0,
+            )
+        else:
+            a = got_ref[:, cols]
+        x = jnp.concatenate([value_ref[:, cols], a], axis=1)
+        half = jnp.dot(x, gate_ref[...], preferred_element_type=jnp.float32)
         u = jnp.dot(x, up_ref[...], preferred_element_type=jnp.float32)
-        half = g * 0.5
         h = ((half + half * jnp.tanh(half)) * u).astype(jnp.bfloat16)
         updates.append(jnp.dot(h, down_ref[...], preferred_element_type=jnp.float32))
     for j in range(heads):
         cols = slice(j * DH, (j + 1) * DH)
-        update = updates[j // 2][(j % 2) * tokens : (j % 2 + 1) * tokens]
         head_gate = jax.nn.sigmoid(jnp.full((1, DH), logit_ref[j], jnp.float32))
-        merged = (value_ref[:, cols].astype(jnp.float32) + head_gate * update).astype(jnp.bfloat16)
+        merged = (value_ref[:, cols].astype(jnp.float32) + head_gate * updates[j]).astype(jnp.bfloat16)
         merged_ref[:, cols] = merged
         numer = jnp.dot(weight_ref[j], merged, preferred_element_type=jnp.float32)
         out_ref[:, j * G : (j + 1) * G, :] = part_ref[:, j * G : (j + 1) * G, :] + numer.reshape(
@@ -205,19 +211,27 @@
         send = pl.pallas_call(
             functools.partial(pack_kernel, blocks=blocks, slice_len=slice_len),
             out_shape=near((devices, blocks * slice_len, width + DH), bf16),
-            in_specs=[ANY, VMEM],
+            in_specs=[ANY, ANY],
             scratch_shapes=[
+                pltpu.VMEM(queries.shape, bf16),
                 pltpu.VMEM((heads * G, DH), f32),
                 pltpu.SemaphoreType.DMA((devices, blocks)),
+                pltpu.SemaphoreType.DMA(()),
             ],
             name="pack",
         )(sharer_values, queries)
         got = here(exchange(send))
         mean = pl.pallas_call(
             functools.partial(align_kernel, blocks=blocks, slice_len=slice_len),
-            out_shape=near((devices, blocks * slice_len, width), bf16),
+            out_shape=shape((devices, blocks * slice_len, width), bf16),
             in_specs=[SMEM, SMEM, VMEM],
-            scratch_shapes=[pltpu.VMEM((total, slice_len, width), f32), pltpu.SMEM((total,), jnp.int32)],
+            out_specs=ANY,
+            scratch_shapes=[
+                pltpu.VMEM((devices, blocks * slice_len, width), bf16),
+                pltpu.VMEM((total, slice_len, width), f32),
+                pltpu.SMEM((total,), jnp.int32),
+                pltpu.SemaphoreType.DMA((devices,)),
+            ],
             name="align",
         )(owner, block_slot, got)
         aligned = exchange(mean)

time: 51.7 us -> 50.6 us (0.979)
  Pallas kernels: 13.2 us -> 12.3 us
    pallas_call x1, Pallas kernels: 1.76 us -> 1.09 us  [body(): pl.pallas_call(functools.partial(pack_kernel, blocks=blocks, slice_len=sl...]
where the time goes in v5:
time: 50.6 us; the launch traced here: 50.2 us
  blocking collectives  28.8 us (57%)
  Pallas kernels  12.3 us (24%)
  waiting for transfers between devices  4.95 us (10%)
  starting transfers between devices  3.42 us (7%)
  between operations  0.67 us (1%)
    all_to_all x2, blocking collectives, exchange(): return lax.all_to_all(x, 'ctx', split_axis=0, concat_axis=0, tiled=True)  28.8 us
    pallas_call x1, Pallas kernels, body(): pl.pallas_call(functools.partial(mixer_kernel, blocks=blocks, slice_len=s...  5.39 us
    all_to_all x1, waiting for transfers between devices, exchange(): return lax.all_to_all(x, 'ctx', split_axis=0, concat_axis=0, tiled=True)  4.95 us
    pallas_call x1, Pallas kernels, body(): pl.pallas_call(functools.partial(score_kernel, heads=heads), out_shape=(s...  3.48 us
    all_to_all x1, starting transfers between devices, exchange(): return lax.all_to_all(x, 'ctx', split_axis=0, concat_axis=0, tiled=True)  3.42 us
    pallas_call x1, Pallas kernels, body(): pl.pallas_call(functools.partial(align_kernel, blocks=blocks, slice_len=s...  1.57 us
    pallas_call x1, Pallas kernels, body(): pl.pallas_call(functools.partial(pack_kernel, blocks=blocks, slice_len=sl...  1.09 us
  transfers between devices with their start and end apart: 1, of which 1 were waited for; matrix products, arithmetic and copies ran while one was open for 0% of the time, Pallas kernels for 7%

profile of v5, /device:TPU:0, one launch (start us, length us, event | category | flops | bytes accessed | tf_op | source)
XLA Modules:
  0.0 50.2 jit_solution(17592611531920433872)
XLA Ops:
  0.6 1.1 %pack.1 = bf16[8,32,640]{2,1,0:T(8,128)(2,1)S(1)} custom-call(bf16[256,512]{1,0:T(8,128)(2,1)} %sharer_hbm.1, bf16[1,4096]{1,0:T(2,128)(2,1)} %query_hbm.1), custom_call_target="tpu_custom_call" | custom-call | tf_op jit(solution)/shard_map/pack/pallas_call | solution.py:211
  1.7 18.0 %all_to_all.15.got_ref = bf16[8,32,640]{2,1,0:T(8,128)(2,1)S(1)} all-to-all(bf16[8,32,640]{2,1,0:T(8,128)(2,1)S(1)} %pack.1), channel_id=1, replica_groups=mesh['grp'=2,'ctx'=8,'head'=2] {'ctx'}, dimensions={0} | all-to-all | bytes 655360 | tf_op jit(solution)/shard_map/all_to_all | solution.py:22
  19.7 1.6 %align.1 = bf16[8,32,512]{2,1,0:T(8,128)(2,1)} custom-call(s32[16]{0:T(128)} %bitcast.2, s32[16]{0:T(128)} %slot_ref.1, bf16[8,32,640]{2,1,0:T(8,128)(2,1)S(1)} %all_to_all.15.got_ref), custom_call_target="tpu_custom_call" | custom-call | tf_op jit(solution)/shard_map/align/pallas_call | solution.py:224
  21.3 3.4 %all-to-all-start.1 = ((bf16[8,32,512]{2,1,0:T(8,128)(2,1)}), bf16[8,32,512]{2,1,0:T(8,128)(2,1)S(1)}, u32[]{:S(2)}, u32[]{:S(2)}) async-start(bf16[8,32,512]{2,1,0:T(8,128)(2,1)} %align.1), calls=%async_computation.1 | async-start | bytes 524288 | tf_op jit(solution)/shard_map/all_to_all | solution.py:22
  24.7 3.5 %score.1 = (bf16[4,64,256]{2,1,0:T(8,128)(2,1)}, f32[8,40,128]{2,1,0:T(8,128)}, bf16[256,2048]{1,0:T(8,128)(2,1)S(1)}, bf16[256,2048]{1,0:T(8,128)(2,1)S(1)}, bf16[2048,128]{1,0:T(8,128)(2,1)S(1)}) custom-call(s32[1]{0:T(128)} %bitcast.1.place_ref, bf16[8,32,640]{2,1,0:T(8,128)(2,1)S(1)} %all_to_all.15.got_ref, bf16[256,512]{1,0:T(8,128)(2,1)} %key_ref.1, ...), custom_call_target="tpu_custom_call" | custom-call | flops 16777216 | bytes 2000000 | tf_op jit(solution)/shard_map/score/pallas_call | solution.py:252
  28.2 5.0 %all-to-all-done.1.got_ref = bf16[8,32,512]{2,1,0:T(8,128)(2,1)S(1)} async-done(((bf16[8,32,512]{2,1,0:T(8,128)(2,1)}), bf16[8,32,512]{2,1,0:T(8,128)(2,1)S(1)}, u32[]{:S(2)}, u32[]{:S(2)}) %all-to-all-start.1) | async-done | bytes 262176 | tf_op jit(solution)/shard_map/all_to_all | solution.py:22
  33.2 5.4 %mixer.1 = (bf16[256,512]{1,0:T(8,128)(2,1)}, f32[8,40,128]{2,1,0:T(8,128)S(1)}) custom-call(f32[4]{0:T(128)} %logit_ref.1, bf16[8,32,512]{2,1,0:T(8,128)(2,1)S(1)} %all-to-all-done.1.got_ref, bf16[256,512]{1,0:T(8,128)(2,1)} %value_ref.1, bf16[256,2048]{1,0:T(8,128)(2,1)S(1)} %get-tuple-element.9.gate_ref, bf16[256,2048]{1,0:T(8,128)(2,1)S(1)} %get-tuple-element.10.up_ref, ...), custom_call_target="tpu_custom_call" | custom-call | tf_op jit(solution)/shard_map/mixer/pallas_call | solution.py:272
  38.6 10.9 %all_to_all.16.got_ref = f32[8,40,128]{2,1,0:T(8,128)S(1)} all-to-all(f32[8,40,128]{2,1,0:T(8,128)S(1)} %get-tuple-element.15), channel_id=1, replica_groups=mesh['grp'=2,'ctx'=8,'head'=2] {'ctx'}, dimensions={0} | all-to-all | bytes 327680 | tf_op jit(solution)/shard_map/all_to_all | solution.py:22
  49.4 0.8 %combine.1 = bf16[1,4096]{1,0:T(2,128)(2,1)} custom-call(f32[8,40,128]{2,1,0:T(8,128)S(1)} %all_to_all.16.got_ref), custom_call_target="tpu_custom_call" | custom-call | tf_op jit(solution)/shard_map/combine/pallas_call | solution.py:281
Async XLA Ops:
  21.3 11.9 %all-to-all-start.1 = ((bf16[8,32,512]{2,1,0:T(8,128)(2,1)}), bf16[8,32,512]{2,1,0:T(8,128)(2,1)S(1)}, u32[]{:S(2)}, u32[]{:S(2)}) async-start(bf16[8,32,512]{2,1,0:T(8,128)(2,1)} %align.1), calls=%async_computation.1 | async-start | bytes 524288 | tf_op jit(solution)/shard_map/all_to_all | solution.py:22

commit v6 on v5

--- a/solution.py
+++ b/solution.py
@@ -28,12 +28,20 @@
     return scratch[...].astype(jnp.bfloat16)
 
 
-def pack_kernel(sharer_hbm, query_hbm, out_ref, query_ref, scratch, sems, query_sem, *, blocks, slice_len):
+def pack_kernel(
+    owner_hbm, slot_hbm, sharer_hbm, query_hbm, out_ref, owner_ref, slot_ref, query_ref, scratch, sems, query_sem,
+    place_sems, *, blocks, slice_len
+):
     devices = out_ref.shape[0]
+    copies = [
+        pltpu.make_async_copy(owner_hbm, owner_ref, place_sems.at[0]),
+        pltpu.make_async_copy(slot_hbm, slot_ref, place_sems.at[1]),
+    ]
+    for copy in copies:
+        copy.start()
     query_copy = pltpu.make_async_copy(query_hbm, query_ref, query_sem)
     query_copy.start()
     width = sharer_hbm.shape[1]
-    copies = []
     for d in range(devices):
         for k in range(blocks):
             copies.append(
@@ -208,18 +216,24 @@
         return pltpu.with_memory_space_constraint(x, pltpu.VMEM) if tiled else x
 
     if tiled:
-        send = pl.pallas_call(
+        send, owner_s, slot_s = pl.pallas_call(
             functools.partial(pack_kernel, blocks=blocks, slice_len=slice_len),
-            out_shape=near((devices, blocks * slice_len, width + DH), bf16),
-            in_specs=[ANY, ANY],
+            out_shape=(
+                near((devices, blocks * slice_len, width + DH), bf16),
+                pltpu.SMEM((total,), jnp.int32),
+                pltpu.SMEM((total,), jnp.int32),
+            ),
+            in_specs=[ANY] * 4,
+            out_specs=(VMEM, SMEM, SMEM),
             scratch_shapes=[
                 pltpu.VMEM(queries.shape, bf16),
                 pltpu.VMEM((heads * G, DH), f32),
                 pltpu.SemaphoreType.DMA((devices, blocks)),
                 pltpu.SemaphoreType.DMA(()),
+                pltpu.SemaphoreType.DMA((2,)),
             ],
             name="pack",
-        )(sharer_values, queries)
+        )(owner, block_slot, sharer_values, queries)
         got = here(exchange(send))
         mean = pl.pallas_call(
             functools.partial(align_kernel, blocks=blocks, slice_len=slice_len),
@@ -233,7 +247,11 @@
                 pltpu.SemaphoreType.DMA((devices,)),
             ],
             name="align",
-        )(owner, block_slot, got)
+        )(
+            pltpu.with_memory_space_constraint(owner_s, pltpu.SMEM),
+            pltpu.with_memory_space_constraint(slot_s, pltpu.SMEM),
+            got,
+        )
         aligned = exchange(mean)
         asked = got
     else:

time: 50.6 us -> 50 us (0.988)
  Pallas kernels: 12.3 us -> 11.7 us
    pallas_call x1, Pallas kernels: 1.57 us -> 0.9 us  [body(): pl.pallas_call(functools.partial(align_kernel, blocks=blocks, slice_len=s...]
where the time goes in v6:
time: 50 us; the launch traced here: 49.6 us
  blocking collectives  28.8 us (58%)
  Pallas kernels  11.7 us (23%)
  waiting for transfers between devices  4.96 us (10%)
  starting transfers between devices  3.42 us (7%)
  between operations  0.67 us (1%)
    all_to_all x2, blocking collectives, exchange(): return lax.all_to_all(x, 'ctx', split_axis=0, concat_axis=0, tiled=True)  28.8 us
    pallas_call x1, Pallas kernels, body(): pl.pallas_call(functools.partial(mixer_kernel, blocks=blocks, slice_len=s...  5.39 us
    all_to_all x1, waiting for transfers between devices, exchange(): return lax.all_to_all(x, 'ctx', split_axis=0, concat_axis=0, tiled=True)  4.96 us
    pallas_call x1, Pallas kernels, body(): pl.pallas_call(functools.partial(score_kernel, heads=heads), out_shape=(s...  3.48 us
    all_to_all x1, starting transfers between devices, exchange(): return lax.all_to_all(x, 'ctx', split_axis=0, concat_axis=0, tiled=True)  3.42 us
    pallas_call x1, Pallas kernels, body(): pl.pallas_call(functools.partial(pack_kernel, blocks=blocks, slice_len=sl...  1.13 us
  transfers between devices with their start and end apart: 1, of which 1 were waited for; matrix products, arithmetic and copies ran while one was open for 0% of the time, Pallas kernels for 7%

profile of v6, /device:TPU:0, one launch (start us, length us, event | category | flops | bytes accessed | tf_op | source)
XLA Modules:
  0.0 49.6 jit_solution(3190288776467710514)
XLA Ops:
  0.6 1.1 %pack.1 = (bf16[8,32,640]{2,1,0:T(8,128)(2,1)S(1)}, s32[16]{0:T(128)S(4)}, s32[16]{0:T(128)S(4)}) custom-call(s32[16]{0:T(128)} %bitcast.2, s32[16]{0:T(128)} %slot_hbm.1, bf16[256,512]{1,0:T(8,128)(2,1)} %sharer_hbm.1, bf16[1,4096]{1,0:T(2,128)(2,1)} %query_hbm.1), custom_call_target="tpu_custom_call" | custom-call | tf_op jit(solution)/shard_map/pack/pallas_call | solution.py:219
  1.8 18.0 %all_to_all.15.got_ref = bf16[8,32,640]{2,1,0:T(8,128)(2,1)S(1)} all-to-all(bf16[8,32,640]{2,1,0:T(8,128)(2,1)S(1)} %get-tuple-element.14), channel_id=1, replica_groups=mesh['grp'=2,'ctx'=8,'head'=2] {'ctx'}, dimensions={0} | all-to-all | bytes 655360 | tf_op jit(solution)/shard_map/all_to_all | solution.py:22
  19.8 0.9 %align.1 = bf16[8,32,512]{2,1,0:T(8,128)(2,1)} custom-call(s32[16]{0:T(128)S(4)} %get-tuple-element.12.owner_ref, s32[16]{0:T(128)S(4)} %get-tuple-element.13.slot_ref, bf16[8,32,640]{2,1,0:T(8,128)(2,1)S(1)} %all_to_all.15.got_ref), custom_call_target="tpu_custom_call" | custom-call | tf_op jit(solution)/shard_map/align/pallas_call | solution.py:238
  20.7 3.4 %all-to-all-start.1 = ((bf16[8,32,512]{2,1,0:T(8,128)(2,1)}), bf16[8,32,512]{2,1,0:T(8,128)(2,1)S(1)}, u32[]{:S(2)}, u32[]{:S(2)}) async-start(bf16[8,32,512]{2,1,0:T(8,128)(2,1)} %align.1), calls=%async_computation.1 | async-start | bytes 524288 | tf_op jit(solution)/shard_map/all_to_all | solution.py:22
  24.1 3.5 %score.1 = (bf16[4,64,256]{2,1,0:T(8,128)(2,1)}, f32[8,40,128]{2,1,0:T(8,128)}, bf16[256,2048]{1,0:T(8,128)(2,1)S(1)}, bf16[256,2048]{1,0:T(8,128)(2,1)S(1)}, bf16[2048,128]{1,0:T(8,128)(2,1)S(1)}) custom-call(s32[1]{0:T(128)} %bitcast.1.place_ref, bf16[8,32,640]{2,1,0:T(8,128)(2,1)S(1)} %all_to_all.15.got_ref, bf16[256,512]{1,0:T(8,128)(2,1)} %key_ref.1, ...), custom_call_target="tpu_custom_call" | custom-call | flops 16777216 | bytes 2000000 | tf_op jit(solution)/shard_map/score/pallas_call | solution.py:270
  27.6 5.0 %all-to-all-done.1.got_ref = bf16[8,32,512]{2,1,0:T(8,128)(2,1)S(1)} async-done(((bf16[8,32,512]{2,1,0:T(8,128)(2,1)}), bf16[8,32,512]{2,1,0:T(8,128)(2,1)S(1)}, u32[]{:S(2)}, u32[]{:S(2)}) %all-to-all-start.1) | async-done | bytes 262176 | tf_op jit(solution)/shard_map/all_to_all | solution.py:22
  32.5 5.4 %mixer.1 = (bf16[256,512]{1,0:T(8,128)(2,1)}, f32[8,40,128]{2,1,0:T(8,128)S(1)}) custom-call(f32[4]{0:T(128)} %logit_ref.1, bf16[8,32,512]{2,1,0:T(8,128)(2,1)S(1)} %all-to-all-done.1.got_ref, bf16[256,512]{1,0:T(8,128)(2,1)} %value_ref.1, bf16[256,2048]{1,0:T(8,128)(2,1)S(1)} %get-tuple-element.15.gate_ref, bf16[256,2048]{1,0:T(8,128)(2,1)S(1)} %get-tuple-element.16.up_ref, ...), custom_call_target="tpu_custom_call" | custom-call | tf_op jit(solution)/shard_map/mixer/pallas_call | solution.py:290
  37.9 10.9 %all_to_all.16.got_ref = f32[8,40,128]{2,1,0:T(8,128)S(1)} all-to-all(f32[8,40,128]{2,1,0:T(8,128)S(1)} %get-tuple-element.21), channel_id=1, replica_groups=mesh['grp'=2,'ctx'=8,'head'=2] {'ctx'}, dimensions={0} | all-to-all | bytes 327680 | tf_op jit(solution)/shard_map/all_to_all | solution.py:22
  48.8 0.8 %combine.1 = bf16[1,4096]{1,0:T(2,128)(2,1)} custom-call(f32[8,40,128]{2,1,0:T(8,128)S(1)} %all_to_all.16.got_ref), custom_call_target="tpu_custom_call" | custom-call | tf_op jit(solution)/shard_map/combine/pallas_call | solution.py:299
Async XLA Ops:
  20.7 11.9 %all-to-all-start.1 = ((bf16[8,32,512]{2,1,0:T(8,128)(2,1)}), bf16[8,32,512]{2,1,0:T(8,128)(2,1)S(1)}, u32[]{:S(2)}, u32[]{:S(2)}) async-start(bf16[8,32,512]{2,1,0:T(8,128)(2,1)} %align.1), calls=%async_computation.1 | async-start | bytes 524288 | tf_op jit(solution)/shard_map/all_to_all | solution.py:22

commit v7 on v6

--- a/solution.py
+++ b/solution.py
@@ -144,8 +144,8 @@
 
 
 def mixer_kernel(
-    logit_ref, got_ref, value_ref, gate_ref, up_ref, down_ref, weight_ref, part_ref, merged_ref, out_ref,
-    *, blocks, slice_len
+    logit_ref, got_ref, value_ref, gate_ref, up_ref, down_ref, weight_ref, part_ref, merged_hbm, out_ref,
+    merged_ref, sems, *, blocks, slice_len
 ):
     heads = value_ref.shape[1] // DH
     rows = part_ref.shape[0]
@@ -169,15 +169,23 @@
         u = jnp.dot(x, up_ref[...], preferred_element_type=jnp.float32)
         h = ((half + half * jnp.tanh(half)) * u).astype(jnp.bfloat16)
         updates.append(jnp.dot(h, down_ref[...], preferred_element_type=jnp.float32))
+    copies = []
     for j in range(heads):
         cols = slice(j * DH, (j + 1) * DH)
         head_gate = jax.nn.sigmoid(jnp.full((1, DH), logit_ref[j], jnp.float32))
         merged = (value_ref[:, cols].astype(jnp.float32) + head_gate * updates[j]).astype(jnp.bfloat16)
         merged_ref[:, cols] = merged
+        head = pl.ds(j * DH, DH)
+        copies.append(
+            pltpu.make_async_copy(merged_ref.at[:, head], merged_hbm.at[:, head], sems.at[j])
+        )
+        copies[-1].start()
         numer = jnp.dot(weight_ref[j], merged, preferred_element_type=jnp.float32)
         out_ref[:, j * G : (j + 1) * G, :] = part_ref[:, j * G : (j + 1) * G, :] + numer.reshape(
             rows, G, DH
         )
+    for copy in copies:
+        copy.wait()
 
 
 def combine_kernel(got_ref, out_ref, scratch, *, heads):
@@ -291,6 +299,11 @@
         functools.partial(mixer_kernel, blocks=blocks, slice_len=slice_len if tiled else 0),
         out_shape=(shape((tokens, width), bf16), near(part.shape, f32)),
         in_specs=[SMEM] + [VMEM] * 7,
+        out_specs=(ANY, VMEM),
+        scratch_shapes=[
+            pltpu.VMEM((tokens, width), bf16),
+            pltpu.SemaphoreType.DMA((heads,)),
+        ],
         name="mixer",
     )(
         gate_logit, here(aligned), recv_values, here(gate_v), here(up_v), here(down_v),

time: 50 us -> 50 us (level)
  no operation moved by 1% of the time
where the time goes in v7:
time: 50 us; the launch traced here: 49.5 us
  blocking collectives  28.9 us (58%)
  Pallas kernels  11.6 us (23%)
  waiting for transfers between devices  4.96 us (10%)
  starting transfers between devices  3.42 us (7%)
  between operations  0.68 us (1%)
    all_to_all x2, blocking collectives, exchange(): return lax.all_to_all(x, 'ctx', split_axis=0, concat_axis=0, tiled=True)  28.9 us
    pallas_call x1, Pallas kernels, body(): pl.pallas_call(functools.partial(mixer_kernel, blocks=blocks, slice_len=s...  5.35 us
    all_to_all x1, waiting for transfers between devices, exchange(): return lax.all_to_all(x, 'ctx', split_axis=0, concat_axis=0, tiled=True)  4.96 us
    pallas_call x1, Pallas kernels, body(): pl.pallas_call(functools.partial(score_kernel, heads=heads), out_shape=(s...  3.48 us
    all_to_all x1, starting transfers between devices, exchange(): return lax.all_to_all(x, 'ctx', split_axis=0, concat_axis=0, tiled=True)  3.42 us
    pallas_call x1, Pallas kernels, body(): pl.pallas_call(functools.partial(pack_kernel, blocks=blocks, slice_len=sl...  1.13 us
  transfers between devices with their start and end apart: 1, of which 1 were waited for; matrix products, arithmetic and copies ran while one was open for 0% of the time, Pallas kernels for 7%

profile of v7, /device:TPU:0, one launch (start us, length us, event | category | flops | bytes accessed | tf_op | source)
XLA Modules:
  0.0 49.5 jit_solution(11579833424661421215)
XLA Ops:
  0.6 1.1 %pack.1 = (bf16[8,32,640]{2,1,0:T(8,128)(2,1)S(1)}, s32[16]{0:T(128)S(4)}, s32[16]{0:T(128)S(4)}) custom-call(s32[16]{0:T(128)} %bitcast.2, s32[16]{0:T(128)} %slot_hbm.1, bf16[256,512]{1,0:T(8,128)(2,1)} %sharer_hbm.1, bf16[1,4096]{1,0:T(2,128)(2,1)} %query_hbm.1), custom_call_target="tpu_custom_call" | custom-call | tf_op jit(solution)/shard_map/pack/pallas_call | solution.py:227
  1.8 18.0 %all_to_all.15.got_ref = bf16[8,32,640]{2,1,0:T(8,128)(2,1)S(1)} all-to-all(bf16[8,32,640]{2,1,0:T(8,128)(2,1)S(1)} %get-tuple-element.14), channel_id=1, replica_groups=mesh['grp'=2,'ctx'=8,'head'=2] {'ctx'}, dimensions={0} | all-to-all | bytes 655360 | tf_op jit(solution)/shard_map/all_to_all | solution.py:22
  19.8 0.9 %align.1 = bf16[8,32,512]{2,1,0:T(8,128)(2,1)} custom-call(s32[16]{0:T(128)S(4)} %get-tuple-element.12.owner_ref, s32[16]{0:T(128)S(4)} %get-tuple-element.13.slot_ref, bf16[8,32,640]{2,1,0:T(8,128)(2,1)S(1)} %all_to_all.15.got_ref), custom_call_target="tpu_custom_call" | custom-call | tf_op jit(solution)/shard_map/align/pallas_call | solution.py:246
  20.7 3.4 %all-to-all-start.1 = ((bf16[8,32,512]{2,1,0:T(8,128)(2,1)}), bf16[8,32,512]{2,1,0:T(8,128)(2,1)S(1)}, u32[]{:S(2)}, u32[]{:S(2)}) async-start(bf16[8,32,512]{2,1,0:T(8,128)(2,1)} %align.1), calls=%async_computation.1 | async-start | bytes 524288 | tf_op jit(solution)/shard_map/all_to_all | solution.py:22
  24.1 3.5 %score.1 = (bf16[4,64,256]{2,1,0:T(8,128)(2,1)}, f32[8,40,128]{2,1,0:T(8,128)}, bf16[256,2048]{1,0:T(8,128)(2,1)S(1)}, bf16[256,2048]{1,0:T(8,128)(2,1)S(1)}, bf16[2048,128]{1,0:T(8,128)(2,1)S(1)}) custom-call(s32[1]{0:T(128)} %bitcast.1.place_ref, bf16[8,32,640]{2,1,0:T(8,128)(2,1)S(1)} %all_to_all.15.got_ref, bf16[256,512]{1,0:T(8,128)(2,1)} %key_ref.1, ...), custom_call_target="tpu_custom_call" | custom-call | flops 16777216 | bytes 2000000 | tf_op jit(solution)/shard_map/score/pallas_call | solution.py:278
  27.6 5.0 %all-to-all-done.1.got_ref = bf16[8,32,512]{2,1,0:T(8,128)(2,1)S(1)} async-done(((bf16[8,32,512]{2,1,0:T(8,128)(2,1)}), bf16[8,32,512]{2,1,0:T(8,128)(2,1)S(1)}, u32[]{:S(2)}, u32[]{:S(2)}) %all-to-all-start.1) | async-done | bytes 262176 | tf_op jit(solution)/shard_map/all_to_all | solution.py:22
  32.5 5.3 %mixer.1 = (bf16[256,512]{1,0:T(8,128)(2,1)}, f32[8,40,128]{2,1,0:T(8,128)S(1)}) custom-call(f32[4]{0:T(128)} %logit_ref.1, bf16[8,32,512]{2,1,0:T(8,128)(2,1)S(1)} %all-to-all-done.1.got_ref, bf16[256,512]{1,0:T(8,128)(2,1)} %value_ref.1, bf16[256,2048]{1,0:T(8,128)(2,1)S(1)} %get-tuple-element.15.gate_ref, bf16[256,2048]{1,0:T(8,128)(2,1)S(1)} %get-tuple-element.16.up_ref, ...), custom_call_target="tpu_custom_call" | custom-call | tf_op jit(solution)/shard_map/mixer/pallas_call | solution.py:298
  37.9 10.9 %all_to_all.16.got_ref = f32[8,40,128]{2,1,0:T(8,128)S(1)} all-to-all(f32[8,40,128]{2,1,0:T(8,128)S(1)} %get-tuple-element.21), channel_id=1, replica_groups=mesh['grp'=2,'ctx'=8,'head'=2] {'ctx'}, dimensions={0} | all-to-all | bytes 327680 | tf_op jit(solution)/shard_map/all_to_all | solution.py:22
  48.8 0.8 %combine.1 = bf16[1,4096]{1,0:T(2,128)(2,1)} custom-call(f32[8,40,128]{2,1,0:T(8,128)S(1)} %all_to_all.16.got_ref), custom_call_target="tpu_custom_call" | custom-call | tf_op jit(solution)/shard_map/combine/pallas_call | solution.py:312
Async XLA Ops:
  20.7 11.9 %all-to-all-start.1 = ((bf16[8,32,512]{2,1,0:T(8,128)(2,1)}), bf16[8,32,512]{2,1,0:T(8,128)(2,1)S(1)}, u32[]{:S(2)}, u32[]{:S(2)}) async-start(bf16[8,32,512]{2,1,0:T(8,128)(2,1)} %align.1), calls=%async_computation.1 | async-start | bytes 524288 | tf_op jit(solution)/shard_map/all_to_all | solution.py:22
